TPU v7x, 128 devices: a whole 4x4x4 slice. The times are simulated.
128 devices in a mesh: dp: 16 (over x_lo, y, core), layer: 8 (over x_hi, z).
Axes of the slice: x: 4 (x_hi: 2, x_lo: 2; x = x_hi * 2 + x_lo), y: 4, z: 4, core: 2. Of those that a mesh axis runs over, the one named last changes fastest.
Arguments:
- activations: bfloat16 [4096, 8, 7168], P('dp', 'layer'), may hold values from -200 to 200
- labels: int32 [4096], P('dp'), may hold values from 0 to 511
- weights: float32 [7168, 8, 512], P('dp', 'layer'), may hold values from -0.0625 to 0.0625
- first_moment: float32 [7168, 8, 512], P('dp', 'layer'), may hold values from -0.00036621094 to 0.00036621094
- second_moment: float32 [7168, 8, 512], P('dp', 'layer'), may hold values from 2.1287373e-12 to 2.1287373e-11
Outputs:
- new_weights: float32 [7168, 8, 512], P('dp', 'layer')
- new_first: float32 [7168, 8, 512], P('dp', 'layer')
- new_second: float32 [7168, 8, 512], P('dp', 'layer')
- loss: float32 [], replicated
All inputs are finite; a program needn't handle non-finite values.
Results may differ from a plain program's by a relative error of at most 0.0014.
Values may be sent and summed in bfloat16 or wider, within the bound.
A program may use at most 128 MiB of HBM per device.

v0:
```python
import functools

import jax
import jax.numpy as jnp
from jax import lax
from jax.sharding import Mesh
from jax.sharding import PartitionSpec as P

STEP = 10
DP = ("dp_0", "dp_1", "dp_2")
LAYER = ("layer_0", "layer_1")
DP_LAYER = ("dp_0", "dp_1", "dp_2", "layer_0", "layer_1")


def one_axis_at_a_time(shard, axes):
    return functools.reduce(lax.psum, axes, shard)


def shards(activations, labels, weights, first_moment, second_moment):
    tok_rows = activations.shape[0]
    local_layers = activations.shape[1]
    tokens = tok_rows * lax.axis_size(DP)
    layers = local_layers * lax.axis_size(LAYER)
    width = weights.shape[2]
    low_weights = weights.astype(jnp.bfloat16)
    block = activations
    logits = jnp.einsum(
        "tlk,klc->ltc",
        block,
        lax.all_gather(low_weights, DP, axis=0, tiled=True),
        preferred_element_type=jnp.float32,
    )
    top = jnp.max(logits, axis=2, keepdims=True)
    exps = jnp.exp(logits - top)
    denom = jnp.sum(exps, axis=2, keepdims=True)
    classes = jnp.arange(width, dtype=jnp.int32)
    onehot = (labels[None, :, None] == classes[None, None, :]).astype(jnp.float32)
    picked = jnp.sum(logits * onehot, axis=2)
    local_loss = jnp.sum(top[:, :, 0] + jnp.log(denom[:, :, 0]) - picked)
    probs = exps / denom
    slope = ((probs - onehot) / tokens).astype(jnp.bfloat16)
    total = one_axis_at_a_time(local_loss, DP_LAYER)
    regrouped = lax.all_to_all(activations, DP, split_axis=2, concat_axis=0, tiled=True)
    block = regrouped
    grad = jnp.einsum(
        "tlk,ltc->klc",
        block,
        lax.all_gather(slope, DP, axis=1, tiled=True),
        preferred_element_type=jnp.float32,
    )
    local_square = jnp.sum(grad * grad)
    square = one_axis_at_a_time(local_square, DP_LAYER)
    loss = total / (tokens * layers)
    factor = jnp.minimum(1.0, 0.25 / jnp.sqrt(square + 1e-12))
    clipped = factor * grad
    new_first = 0.9 * first_moment + 0.1 * clipped
    new_second = 0.999 * second_moment + 0.001 * clipped * clipped
    new_weights = weights - 0.001 * (new_first / (1.0 - 0.9**STEP)) / (
        jnp.sqrt(new_second / (1.0 - 0.999**STEP)) + 1e-08
    )
    return (new_weights, new_first, new_second, loss)


def solution(mesh):
    finer = Mesh(
        mesh.devices.reshape(2, 4, 2, 2, 4), ("dp_0", "dp_1", "dp_2", "layer_0", "layer_1")
    )
    in_specs = (
        P(DP, LAYER, None),
        P(DP),
        P(DP, LAYER, None),
        P(DP, LAYER, None),
        P(DP, LAYER, None),
    )
    out_specs = (P(DP, LAYER, None), P(DP, LAYER, None), P(DP, LAYER, None), P())
    return jax.shard_map(
        shards, mesh=finer, in_specs=in_specs, out_specs=out_specs, check_vma=False
    )
```

profile of v0, /device:TPU:1, one launch (start us, length us, event | category | flops | bytes accessed | tf_op | source)
XLA Modules:
  0.0 259.4 jit_solution(9206150363318013744)
XLA Ops:
  7.2 0.0 all-gather.4.cloned.1.call-start
  7.2 2.0 copy.43
  9.2 0.0 all-gather.4.cloned.1.call-update
  9.2 0.0 copy-start.3
  9.3 0.0 all-gather.6.cloned.1.call-start
  9.3 51.7 %all-gather.4.cloned.1.call-done = bf16[7168,1,512]{2,0,1:T(8,128)(2,1)} async-done(((bf16[448,1,512]{2,0,1:T(8,128)(2,1)}), bf16[7168,1,512]{2,0,1:T(8,128)(2,1)}) %all-gather.4.cloned.1.call-update) | async-done | bytes 7340048 | tf_op jit(solution)/shard_map/all_gather | solution.py:30
  61.0 6.3 %fusion.8 = (f32[256]{0:T(256)S(1)}, f32[256,512]{1,0:T(8,128)S(1)}) fusion(bf16[7168,1,512]{2,0,1:T(8,128)(2,1)} %all-gather.4.cloned.1.call-done, bf16[256,1,7168]{2,0,1:T(8,128)(2,1)} %param.5), kind=kOutput, calls=%fused_computation.18 | convolution fusion | flops 1879179008 | bytes 11535360 | tf_op jit(solution)/shard_map/tlk,klc->ltc/dot_general | solution.py:27
  67.3 0.0 copy-done.3
  67.3 0.3 select_reduce_fusion
  67.6 0.9 multiply_convert_fusion
  68.6 0.0 all-gather.6.cloned.1.call-update
  68.6 16.4 %copy.25 = bf16[256,1,7168]{0,1,2:T(2,128)(2,1)} copy(bf16[256,1,7168]{2,0,1:T(8,128)(2,1)} %param.5) | data formatting | bytes 7340032 | tf_op args[0]
  85.0 0.5 broadcast.32
  85.5 38.5 %reduce.9 = bf16[7168,256]{1,0:T(8,128)(2,1)} reduce(bf16[7168,1,256]{2,1,0:T(2,128)(2,1)} %bitcast.33, bf16[]{:T(256)} %broadcast.32), dimensions={1}, to_apply=%bitcast.23.reduce_sub_computation | reduce | bytes 7340034
  123.9 10.3 %reshape.68 = bf16[16,2,57344]{2,1,0:T(2,128)(2,1)} reshape(bf16[7168,256]{1,0:T(8,128)(2,1)} %reduce.9) | data formatting | bytes 7340032
  134.2 48.6 %all_to_all.15 = bf16[16,2,57344]{2,1,0:T(2,128)(2,1)} all-to-all(bf16[16,2,57344]{2,1,0:T(2,128)(2,1)} %reshape.68), channel_id=1, replica_groups=mesh['dp_0'=2,'dp_1'=4,'dp_2'=2,'layer_0'=2,'layer_1'=4] {'dp_0','dp_1',..., dimensions={0} | all-to-all | bytes 7340032 | tf_op jit(solution)/shard_map/all_to_all | solution.py:43
  182.8 12.0 %reshape.69 = bf16[7168,1,256]{2,1,0:T(2,128)(2,1)} reshape(bf16[16,2,57344]{2,1,0:T(2,128)(2,1)} %all_to_all.15) | data formatting | bytes 7340032
  194.8 3.7 %copy.32 = bf16[256,1,7168]{0,2,1:T(8,128)(2,1)S(1)} copy(bf16[256,1,7168]{0,1,2:T(2,128)(2,1)} %bitcast.34) | data formatting | bytes 7340032
  198.5 2.3 copy.33
  200.8 0.6 subtract_reduce_fusion
  201.4 0.0 all-gather.6.cloned.1.call-done
  201.4 0.0 copy-start
  201.4 0.0 copy-start.1
  201.4 0.0 copy-start.2
  201.4 7.0 %multiply_reduce_fusion = (f32[]{:T(128)}, f32[512,448]{0,1:T(8,128)}) fusion(bf16[4096,448]{0,1:T(8,128)(2,1)} %bitcast.36, bf16[4096,512]{1,0:T(8,128)(2,1)} %all-gather.6.cloned.1.call-done), kind=kOutput, calls=%fused_computation.10 | convolution fusion | flops 1879506944 | bytes 8781828 | tf_op jit(solution)/shard_map/tlk,ltc->klc/dot_general | solution.py:45
  208.4 4.4 %all-reduce.4 = (f32[]{:T(128)}, f32[]{:T(128)}) all-reduce(f32[]{:T(128)} %get-tuple-element.33, f32[]{:T(128)} %subtract_reduce_fusion), channel_id=1, replica_groups=mesh['dp_0'=2,'dp_1'=4,'dp_2'=2,'layer_0'=2,'layer_1'=4] {'dp_0'}, use_global_device_ids=true, to_apply=%region_3.0 | all-reduce | flops 2 | bytes 16 | tf_op jit(solution)/shard_map/psum | solution.py:16
  212.8 8.4 %all-reduce.1 = (f32[]{:T(128)}, f32[]{:T(128)}) all-reduce(f32[]{:T(128)} %get-tuple-element.26, f32[]{:T(128)} %get-tuple-element.27), channel_id=1, replica_groups=mesh['dp_0'=2,'dp_1'=4,'dp_2'=2,'layer_0'=2,'layer_1'=4] {'dp_1'}, use_global_device_ids=true, to_apply=%region_4.0 | all-reduce | flops 2 | bytes 16 | tf_op jit(solution)/shard_map/psum | solution.py:16
  221.2 6.0 %all-reduce.3 = (f32[]{:T(128)}, f32[]{:T(128)}) all-reduce(f32[]{:T(128)} %get-tuple-element.20, f32[]{:T(128)} %get-tuple-element.21), channel_id=1, replica_groups=mesh['dp_0'=2,'dp_1'=4,'dp_2'=2,'layer_0'=2,'layer_1'=4] {'dp_2'}, use_global_device_ids=true, to_apply=%region_5.0 | all-reduce | flops 2 | bytes 16 | tf_op jit(solution)/shard_map/psum | solution.py:16
  227.2 5.9 %all-reduce.2 = (f32[]{:T(128)}, f32[]{:T(128)}) all-reduce(f32[]{:T(128)} %get-tuple-element.24, f32[]{:T(128)} %get-tuple-element.25), channel_id=1, replica_groups=mesh['dp_0'=2,'dp_1'=4,'dp_2'=2,'layer_0'=2,'layer_1'=4] {'layer_0'}, use_global_device_ids=true, to_apply=%region_6.0 | all-reduce | flops 2 | bytes 16 | tf_op jit(solution)/shard_map/psum | solution.py:16
  233.1 9.5 %all-reduce = (f32[]{:T(128)}, f32[]{:T(128)}) all-reduce(f32[]{:T(128)} %get-tuple-element.22, f32[]{:T(128)} %get-tuple-element.23), channel_id=1, replica_groups=mesh['dp_0'=2,'dp_1'=4,'dp_2'=2,'layer_0'=2,'layer_1'=4] {'layer_1'}, use_global_device_ids=true, to_apply=%region_7.0 | all-reduce | flops 2 | bytes 16 | tf_op jit(solution)/shard_map/psum | solution.py:16
  243.3 0.0 copy-done
  243.3 0.0 copy-done.1
  243.4 0.0 copy-done.2
  243.4 1.8 divide_subtract_fusion
  245.2 1.9 copy.29
  247.1 1.9 copy.30
  248.9 1.9 copy.31
Async XLA Ops:
  7.2 53.8 %all-gather.4.cloned.1.call-start = ((), (), s32[]{:S(2)}) async-start(), calls=%async_computation.1 | async-start | bytes 7798784 | tf_op jit(solution)/shard_map/all_gather | solution.py:30
  9.2 58.1 %copy-start.3 = (s32[256]{0:T(256)S(1)}, s32[256]{0:T(256)}, u32[]{:S(2)}) copy-start(s32[256]{0:T(256)} %param.6) | copy-start | bytes 3076
  9.3 192.1 %all-gather.6.cloned.1.call-start = ((), (), s32[]{:S(2)}) async-start(), calls=%async_computation.2 | async-start | bytes 4456448 | tf_op jit(solution)/shard_map/all_gather | solution.py:48
  201.4 41.9 %copy-start = (f32[448,1,512]{2,1,0:T(1,128)S(1)}, f32[448,1,512]{2,1,0:T(1,128)}, u32[]{:S(2)}) copy-start(f32[448,1,512]{2,1,0:T(1,128)} %param.7) | copy-start | bytes 2752516
  201.4 41.9 %copy-start.1 = (f32[448,1,512]{2,1,0:T(1,128)S(1)}, f32[448,1,512]{2,1,0:T(1,128)}, u32[]{:S(2)}) copy-start(f32[448,1,512]{2,1,0:T(1,128)} %param.8) | copy-start | bytes 2752516
  201.4 42.0 %copy-start.2 = (f32[448,1,512]{2,1,0:T(1,128)S(1)}, f32[448,1,512]{2,1,0:T(1,128)}, u32[]{:S(2)}) copy-start(f32[448,1,512]{2,1,0:T(1,128)} %param.9) | copy-start | bytes 2752516
Sparse Core Ops, SparseCore 0:
  10.2 50.6 all-gather.3
  68.7 38.1 all-gather.5
where the time goes:
time: 263 us; the launch traced here: 259 us
  blocking collectives  82.8 us (31%)
  local copies, waits for them, and re-layouts  52.8 us (20%)
  waiting for transfers between devices  51.7 us (20%)
  other arithmetic  42.1 us (16%)
  between operations  16.6 us (6%)
  matrix products  13.3 us (5%)
    unnamed x18, local copies, waits for them, and re-layouts  52.8 us
    all_gather x1, waiting for transfers between devices, shards(): lax.all_gather(low_weights, DP, axis=0, tiled=True)  51.7 us
    all_to_all x1, blocking collectives, shards(): lax.all_to_all(activations, DP, split_axis=2, concat_axis=0, tiled=True)  48.6 us
    unnamed x1, other arithmetic  38.5 us
    psum x5, blocking collectives, one_axis_at_a_time(): return functools.reduce(lax.psum, axes, shard)  34.2 us
    dot_general x1, matrix products, shards(): jnp.einsum('tlk,ltc->klc', block, lax.all_gather(slope, DP, axis=1, tiled...  7.02 us
    dot_general x1, matrix products, shards(): jnp.einsum('tlk,klc->ltc', block, lax.all_gather(low_weights, DP, axis=0,...  6.33 us
  transfers between devices with their start and end apart: 2, of which 1 were waited for; matrix products, arithmetic and copies ran while one was open for 32% of the time, Pallas kernels for 0%

commit v1 on v0

v1 whole, which is shorter than its diff:
```python
import jax
import jax.numpy as jnp
from jax import lax
from jax.experimental import pallas as pl
from jax.experimental.pallas import tpu as pltpu
from jax.sharding import PartitionSpec as P

STEP = 10
BF16 = jnp.bfloat16
F32 = jnp.float32
MESH = pl.DeviceIdType.MESH


def kernel(
    tokens,
    a_hbm,
    labels_ref,
    w_hbm,
    grad_ref,
    sums_ref,
    a_v,
    w32,
    wbuf,
    arx,
    slopes,
    acc,
    part,
    dbuf,
    xsend,
    xrecv,
    slots1,
    slots2,
    ld_sem,
    ws_sem,
    wr_sem,
    ds_sem,
    dr_sem,
    as_sem,
    ar_sem,
    ss_sem,
    sr_sem,
    es_sem,
    er_sem,
    xs_sem,
    xr_sem,
    p1s,
    p1r,
    p2s,
    p2r,
):
    tok = a_v.shape[0]
    width = wbuf.shape[1]
    rows = wbuf.shape[0] // 16
    half = rows // 2
    chip = 2 * rows
    d = lax.axis_index("dp")
    lay = lax.axis_index("layer")
    x = d // 8
    y = (d // 2) % 4
    c = d % 2

    def dp_of(dx, dy, dc=0):
        return ((x + dx) % 2) * 8 + ((y + dy) % 4) * 2 + (c + dc) % 2

    load_a = pltpu.make_async_copy(a_hbm, a_v, ld_sem.at[0])
    load_w = pltpu.make_async_copy(w_hbm, w32, ld_sem.at[1])
    load_w.start()
    load_a.start()

    barrier = pltpu.get_barrier_semaphore()
    near = [(1, 0, 0), (0, 1, 0), (0, 3, 0), (0, 2, 0), (0, 0, 1)]
    for dx, dy, dc in near:
        pl.semaphore_signal(
            barrier, inc=1, device_id={"dp": dp_of(dx, dy, dc)}, device_id_type=MESH
        )
    for k in range(1, 8):
        pl.semaphore_signal(
            barrier, inc=1, device_id={"layer": (lay + k) % 8}, device_id_type=MESH
        )

    load_w.wait()
    own = pl.multiple_of(d * rows, 64)

    def convert(g, carry):
        for j in range(4):
            v = w32[pl.ds(g * 64 + j, 16, stride=4), :]
            wbuf[pl.ds(pl.multiple_of(own + g * 16, 16), 16), j * 128 : (j + 1) * 128] = v.astype(BF16)
        return carry

    lax.fori_loop(0, rows // 16, convert, 0)
    pl.semaphore_wait(barrier, len(near) + 7)

    sent = []

    def send(src, dst, ssem, rsem, dp):
        cp = pltpu.make_async_remote_copy(
            src_ref=src, dst_ref=dst, send_sem=ssem, recv_sem=rsem,
            device_id={"dp": dp}, device_id_type=MESH,
        )
        cp.start()
        sent.append(cp)
        return cp

    def w_rows(dx, dy, dc, h):
        start = pl.multiple_of(dp_of(dx, dy, dc) * rows + h * half, 32)
        return wbuf.at[pl.ds(start, half), :]

    wcount = [0]

    def w_send(dx, dy, h, tx, ty):
        ref = w_rows(dx, dy, 0, h)
        k = ((dx - tx) % 2) * 4 + (dy - ty) % 4
        i = wcount[0]
        wcount[0] += 1
        send(ref, ref, ws_sem.at[i], wr_sem.at[k, h], dp_of(tx, ty))

    def w_pass(dx, dy, h):
        ref = w_rows(dx, dy, 0, h)
        k = dx * 4 + dy
        send(ref, ref, ds_sem.at[k, h], dr_sem.at[k, h], dp_of(0, 0, 1))

    def w_wait(dx, dy, h):
        ref = w_rows(dx, dy, 0, h)
        pltpu.make_async_remote_copy(
            src_ref=ref, dst_ref=ref, send_sem=ws_sem.at[0], recv_sem=wr_sem.at[dx * 4 + dy, h],
            device_id={"dp": dp_of(0, 0, 1)}, device_id_type=MESH,
        ).wait_recv()

    def d_wait(dx, dy, h):
        ref = w_rows(dx, dy, 1, h)
        pltpu.make_async_remote_copy(
            src_ref=ref, dst_ref=ref, send_sem=ws_sem.at[0], recv_sem=dr_sem.at[dx * 4 + dy, h],
            device_id={"dp": dp_of(0, 0, 1)}, device_id_type=MESH,
        ).wait_recv()

    def a_cols(dx, dy):
        return pl.multiple_of((((x + dx) % 2) * 4 + (y + dy) % 4) * chip, 128)

    def a_send(e, dx, dy):
        send(
            a_hbm.at[:, pl.ds(a_cols(dx, dy), chip)], arx.at[dy - 1, e],
            as_sem.at[dy - 1, e], ar_sem.at[dy - 1, e], dp_of(0, dy),
        )

    def a_wait(e, dy):
        pltpu.make_async_remote_copy(
            src_ref=arx.at[dy - 1, e], dst_ref=arx.at[dy - 1, e],
            send_sem=as_sem.at[dy - 1, e], recv_sem=ar_sem.at[dy - 1, e],
            device_id={"dp": dp_of(0, dy)}, device_id_type=MESH,
        ).wait_recv()

    acc[...] = jnp.zeros_like(acc)

    def logits_of(dx, dy):
        cols = a_cols(dx, dy)
        for h in range(2):
            d_wait(dx, dy, h)

        def step(n, carry):
            lanes = pl.ds(pl.multiple_of(n * 256, 256), 256)
            acc[:, lanes] += jnp.dot(
                a_v[:, pl.ds(cols, chip)], wbuf[pl.ds(cols, chip), lanes],
                preferred_element_type=F32,
            )
            return carry

        lax.fori_loop(0, width // 256, step, 0)

    w_send(0, 0, 0, 1, 0)
    w_send(0, 0, 0, 0, 1)
    w_send(0, 0, 1, 0, 3)
    w_send(0, 0, 1, 1, 0)
    w_send(0, 0, 1, 0, 1)
    w_send(0, 0, 0, 0, 3)
    w_pass(0, 0, 0)
    w_pass(0, 0, 1)
    load_a.wait()

    w_wait(0, 3, 0)
    w_send(0, 3, 0, 0, 1)
    w_send(0, 3, 0, 1, 0)
    w_pass(0, 3, 0)
    w_wait(0, 1, 1)
    w_send(0, 1, 1, 0, 3)
    w_send(0, 1, 1, 1, 0)
    w_pass(0, 1, 1)
    w_wait(1, 0, 0)
    w_send(1, 0, 0, 0, 3)
    w_pass(1, 0, 0)
    w_wait(1, 0, 1)
    w_send(1, 0, 1, 0, 1)
    w_pass(1, 0, 1)
    for dy in (2, 1, 3):
        a_send(0, 1, dy)
    logits_of(0, 0)
    w_wait(0, 3, 1)
    w_pass(0, 3, 1)
    w_wait(0, 1, 0)
    w_pass(0, 1, 0)
    logits_of(1, 0)
    w_wait(0, 2, 0)
    w_send(0, 2, 0, 1, 0)
    w_pass(0, 2, 0)
    w_wait(0, 2, 1)
    w_send(0, 2, 1, 1, 0)
    w_pass(0, 2, 1)
    logits_of(0, 3)
    logits_of(0, 1)
    logits_of(0, 2)
    w_wait(1, 3, 1)
    w_pass(1, 3, 1)
    w_wait(1, 1, 0)
    w_pass(1, 1, 0)
    w_wait(1, 3, 0)
    w_pass(1, 3, 0)
    w_wait(1, 1, 1)
    w_pass(1, 1, 1)
    logits_of(1, 3)
    logits_of(1, 1)
    w_wait(1, 2, 0)
    w_pass(1, 2, 0)
    w_wait(1, 2, 1)
    w_pass(1, 2, 1)
    logits_of(1, 2)

    classes = lax.broadcasted_iota(jnp.int32, (128, width), 1)
    loss_lanes = jnp.zeros((1, 128), F32)
    for t in range(tok // 128):
        lab = jnp.broadcast_to(labels_ref[t : t + 1, :], (128, 128)).T
        lab = jnp.concatenate([lab] * (width // 128), axis=1)
        logits = acc[t * 128 : (t + 1) * 128, :]
        top = jnp.max(logits, axis=1, keepdims=True)
        exps = jnp.exp(logits - top)
        denom = jnp.sum(exps, axis=1, keepdims=True)
        onehot = (lab == classes).astype(F32)
        picked = jnp.sum(logits * onehot, axis=1, keepdims=True)
        probs = exps / denom
        slopes[0, t * 128 : (t + 1) * 128, :] = ((probs - onehot) / tokens).astype(BF16)
        term = top + jnp.log(denom) - picked
        loss_lanes += jnp.sum(jnp.broadcast_to(term, (128, 128)), axis=0, keepdims=True)

    for dy in (2, 1, 3):
        send(slopes.at[0], slopes.at[dy], ss_sem.at[dy - 1], sr_sem.at[dy - 1], dp_of(0, dy))
    for dy in (2, 1, 3):
        a_send(1, 0, dy)

    def s_wait(dy):
        pltpu.make_async_remote_copy(
            src_ref=slopes.at[dy], dst_ref=slopes.at[dy],
            send_sem=ss_sem.at[dy - 1], recv_sem=sr_sem.at[dy - 1],
            device_id={"dp": dp_of(0, dy)}, device_id_type=MESH,
        ).wait_recv()

    def outer(left, right):
        return lax.dot_general(
            left, right, (((0,), (0,)), ((), ())), preferred_element_type=F32
        )

    def accumulate(e, dx, dy, first, start, count):
        at = pl.multiple_of(start, 128)
        if dy == 0:
            left = a_v[:, pl.ds(pl.multiple_of(a_cols(dx, 0) + at, 128), count)]
        else:
            left = arx[dy - 1, e, :, pl.ds(at, count)]
        here = outer(left, slopes[dy])
        if first:
            part[e, pl.ds(at, count), :] = here
        else:
            part[e, pl.ds(at, count), :] += here

    mine = pl.multiple_of(c * rows, 64)
    other = pl.multiple_of((1 - c) * rows, 64)
    big = (1 - c) * 384
    small = c * 512

    def exchange(e, h):
        return send(
            part.at[e, pl.ds(pl.multiple_of(other + h * half, 32), half), :],
            dbuf.at[e, pl.ds(h * half, half), :],
            es_sem.at[e, h], er_sem.at[e, h], dp_of(0, 0, 1),
        )

    accumulate(0, 1, 0, True, big, 512)
    for dy in (1, 3, 2):
        s_wait(dy)
        a_wait(0, dy)
        accumulate(0, 1, dy, False, big, 512)
    swaps = [exchange(0, h) for h in range(2)]
    for dy in (0, 1, 3, 2):
        accumulate(0, 1, dy, dy == 0, small, 384)
    xs = []
    for h in range(2):
        swaps[h].wait_recv()
        piece = pl.ds(h * half, half)
        xsend[piece, :] = part[0, pl.ds(pl.multiple_of(mine + h * half, 32), half), :] + dbuf[0, piece, :]
        xs.append(send(xsend.at[piece, :], xrecv.at[piece, :], xs_sem.at[h], xr_sem.at[h], dp_of(1, 0)))

    for dy in (0, 2, 1, 3):
        if dy:
            a_wait(1, dy)
        accumulate(1, 0, dy, dy == 0, big, 512)
        if dy != 3:
            accumulate(1, 0, dy, dy == 0, small, 384)
    swaps = [exchange(1, h) for h in range(2)]
    accumulate(1, 0, 3, False, small, 384)
    for h in range(2):
        swaps[h].wait_recv()
    for h in range(2):
        xs[h].wait_recv()

    def finish(g, carry):
        r = pl.multiple_of(g * 8, 8)
        m = pl.multiple_of(mine + g * 8, 8)
        for j in range(4):
            lanes = slice(j * 128, (j + 1) * 128)
            v = part[1, pl.ds(m, 8), lanes] + dbuf[1, pl.ds(r, 8), lanes] + xrecv[pl.ds(r, 8), lanes]
            grad_ref[pl.ds(g * 32 + j, 8, stride=4), :] = v
            carry = carry + v * v
        return carry

    square = lax.fori_loop(0, rows // 8, finish, jnp.zeros((8, 128), F32))
    tile = jnp.concatenate(
        [jnp.sum(square, axis=0, keepdims=True), loss_lanes, jnp.zeros((6, 128), F32)], axis=0
    )
    slots1[d] = tile
    first = []
    for k in range(1, 16):
        cp = pltpu.make_async_remote_copy(
            src_ref=slots1.at[d], dst_ref=slots1.at[d], send_sem=p1s.at[k - 1],
            recv_sem=p1r.at[k - 1], device_id={"dp": (d + k) % 16}, device_id_type=MESH,
        )
        cp.start()
        first.append(cp)
    for cp in first:
        cp.wait()
    slots2[lay] = jnp.sum(slots1[...], axis=0)
    second = []
    for k in range(1, 8):
        cp = pltpu.make_async_remote_copy(
            src_ref=slots2.at[lay], dst_ref=slots2.at[lay], send_sem=p2s.at[k - 1],
            recv_sem=p2r.at[k - 1], device_id={"layer": (lay + k) % 8}, device_id_type=MESH,
        )
        cp.start()
        second.append(cp)
    for cp in second:
        cp.wait()
    sums_ref[...] = jnp.sum(slots2[...], axis=0)
    for cp in sent:
        cp.wait_send()


def shards(activations, labels, weights, first_moment, second_moment):
    tok = activations.shape[0]
    depth = activations.shape[2]
    rows, _, width = weights.shape
    tokens = tok * lax.axis_size("dp")
    layers = lax.axis_size("layer")
    dma = pltpu.SemaphoreType.DMA
    vmem = pltpu.VMEM
    lines = rows * width // 128
    anywhere = pl.BlockSpec(memory_space=pl.ANY)
    inside = pl.BlockSpec(memory_space=pltpu.VMEM)

    def body(*refs):
        kernel(tokens, *refs)

    grad, sums = pl.pallas_call(
        body,
        out_shape=(
            jax.ShapeDtypeStruct((lines, 128), F32),
            jax.ShapeDtypeStruct((8, 128), F32),
        ),
        in_specs=[anywhere, inside, anywhere],
        out_specs=(inside, inside),
        scratch_shapes=[
            vmem((tok, depth), BF16),
            vmem((lines, 128), F32),
            vmem((depth, width), BF16),
            vmem((3, 2, tok, 2 * rows), BF16),
            vmem((4, tok, width), BF16),
            vmem((tok, width), F32),
            vmem((2, 2 * rows, width), F32),
            vmem((2, rows, width), F32),
            vmem((rows, width), F32),
            vmem((rows, width), F32),
            vmem((16, 8, 128), F32),
            vmem((8, 8, 128), F32),
            dma((2,)),
            dma((14,)),
            dma((8, 2)),
            dma((8, 2)),
            dma((8, 2)),
            dma((3, 2)),
            dma((3, 2)),
            dma((3,)),
            dma((3,)),
            dma((2, 2)),
            dma((2, 2)),
            dma((2,)),
            dma((2,)),
            dma((15,)),
            dma((15,)),
            dma((7,)),
            dma((7,)),
        ],
        compiler_params=pltpu.CompilerParams(
            collective_id=0, has_side_effects=True, vmem_limit_bytes=48 << 20
        ),
        name="probe_step",
    )(
        activations.reshape(tok, depth),
        labels.reshape(tok // 128, 128),
        weights.reshape(lines, 128),
    )
    square = jnp.sum(sums[0])
    loss = sums[1, 0] / (tokens * layers)
    grad = grad.reshape(rows, 1, width)
    factor = jnp.minimum(1.0, 0.25 / jnp.sqrt(square + 1e-12))
    clipped = factor * grad
    new_first = 0.9 * first_moment + 0.1 * clipped
    new_second = 0.999 * second_moment + 0.001 * clipped * clipped
    new_weights = weights - 0.001 * (new_first / (1.0 - 0.9**STEP)) / (
        jnp.sqrt(new_second / (1.0 - 0.999**STEP)) + 1e-08
    )
    return (new_weights, new_first, new_second, loss)


def solution(mesh):
    rows = P("dp", "layer", None)
    return jax.shard_map(
        shards,
        mesh=mesh,
        in_specs=(rows, P("dp"), rows, rows, rows),
        out_specs=(rows, rows, rows, P()),
        check_vma=False,
    )
```

time: 263 us -> 121 us (0.46); the launches traced: 259 us -> 120 us
  Pallas kernels: 0 us -> 104 us
  blocking collectives: 82.8 us -> 0 us
  waiting for transfers between devices: 51.7 us -> 0 us
  local copies, waits for them, and re-layouts: 52.8 us -> 4.41 us
  other arithmetic: 42.1 us -> 8.44 us
  between operations: 16.6 us -> 3.15 us
  matrix products: 13.3 us -> 0 us
    pallas_call x0 -> x1, Pallas kernels: none -> 104 us  [shards(): pl.pallas_call(body, out_shape=(jax.ShapeDtypeStruct((lines, 128), F32),...]
    all_gather x2 -> x0, waiting for transfers between devices: 51.7 us -> none  [the longest x1 51.7 us: shards(): lax.all_gather(low_weights, DP, axis=0, tiled=True)]
    unnamed x18 -> x10, local copies, waits for them, and re-layouts: 52.8 us -> 3.9 us
    all_to_all x1 -> x0, blocking collectives: 48.6 us -> none  [shards(): lax.all_to_all(activations, DP, split_axis=2, concat_axis=0, tiled=True)]
    unnamed x1 -> x0, other arithmetic: 38.5 us -> none
    psum x5 -> x0, blocking collectives: 34.2 us -> none  [one_axis_at_a_time(): return functools.reduce(lax.psum, axes, shard)]
    dot_general x2 -> x0, matrix products: 13.3 us -> none  [the longest x1 7.02 us: shards(): jnp.einsum('tlk,ltc->klc', block, lax.all_gather(slope, DP, axis=1, tiled...]
    sub x1, other arithmetic: 1.82 us -> 7.78 us  [shards(): weights - 0.001 * (new_first / (1.0 - 0.9 ** STEP)) / (jnp.sqrt(new_secon...]
  transfers between devices with their start and end apart: 2 -> 0, of which waited for: 1 -> 0; matrix products, arithmetic and copies ran while one was open for 32% -> 0% of each run, Pallas kernels for 0% -> 0%
where the time goes in v1:
time: 121 us; the launch traced here: 120 us
  Pallas kernels  104 us (86%)
  other arithmetic  8.44 us (7%)
  local copies, waits for them, and re-layouts  4.41 us (4%)
  between operations  3.15 us (3%)
    pallas_call x1, Pallas kernels, shards(): pl.pallas_call(body, out_shape=(jax.ShapeDtypeStruct((lines, 128), F32),...  104 us
    sub x1, other arithmetic, shards(): weights - 0.001 * (new_first / (1.0 - 0.9 ** STEP)) / (jnp.sqrt(new_secon...  7.78 us
    unnamed x10, local copies, waits for them, and re-layouts  3.9 us

profile of v1, /device:TPU:1, one launch (start us, length us, event | category | flops | bytes accessed | tf_op | source)
XLA Modules:
  0.0 120.4 jit_solution(11545568608080445897)
XLA Ops:
  0.6 0.0 copy-start
  0.6 1.2 copy-done
  1.8 0.0 copy-start.2
  1.8 2.0 %copy-done.2 = bf16[256,1,7168]{2,0,1:T(8,128)(2,1)S(1)} copy-done((bf16[256,1,7168]{2,0,1:T(8,128)(2,1)S(1)}, bf16[256,1,7168]{2,0,1:T(8,128)(2,1)}, u32[]{:S(2)}) %copy-start.2) | copy-done | bytes 3670040
  3.9 0.0 copy-start.3
  3.9 0.7 copy-done.3
  4.5 0.0 copy-start.1
  4.5 0.0 copy-start.4
  4.5 104.4 %probe_step.1 = (f32[1792,128]{1,0:T(8,128)S(1)}, f32[8,128]{1,0:T(8,128)S(1)}) custom-call(bf16[256,7168]{1,0:T(8,128)(2,1)S(1)} %bitcast.6, s32[2,128]{1,0:T(2,128)S(1)} %bitcast.7, f32[1792,128]{1,0:T(8,128)S(1)} %bitcast.5), custom_call_target="tpu_custom_call" | custom-call | tf_op jit(solution)/shard_map/probe_step/pallas_call | solution.py:367
  108.9 0.5 slice.7
  110.1 0.6 slice_reduce_fusion
  111.4 0.1 broadcast_multiply_fusion
  111.5 0.0 copy-done.1
  111.5 0.0 copy-done.4
  111.5 7.8 %divide_subtract_fusion = (f32[448,1,512]{2,1,0:T(1,128)}, f32[448,1,512]{2,1,0:T(1,128)}, f32[448,1,512]{2,1,0:T(1,128)}) fusion(f32[448,1,512]{2,1,0:T(1,128)S(1)} %copy-done.1, f32[448,1,512]{2,1,0:T(1,128)S(1)} %bitcast.8, f32[448,1,512]{2,1,0:T(1,128)S(1)} %copy-done.4, f32[448,1,512]{2,1,0:T(1,128)} %param.9), kind=kLoop, calls=%fused_computation.2 | loop fusion | flops 2752512 | bytes 6422528 | tf_op jit(solution)/shard_map/sub | solution.py:422
Async XLA Ops:
  0.6 1.2 copy-start
  1.8 2.0 %copy-start.2 = (bf16[256,1,7168]{2,0,1:T(8,128)(2,1)S(1)}, bf16[256,1,7168]{2,0,1:T(8,128)(2,1)}, u32[]{:S(2)}) copy-start(bf16[256,1,7168]{2,0,1:T(8,128)(2,1)} %param.5) | copy-start | bytes 11010052
  3.9 0.7 copy-start.3
  4.5 106.9 %copy-start.1 = (f32[448,1,512]{2,1,0:T(1,128)S(1)}, f32[448,1,512]{2,1,0:T(1,128)}, u32[]{:S(2)}) copy-start(f32[448,1,512]{2,1,0:T(1,128)} %param.7) | copy-start | bytes 2752516
  4.5 106.9 %copy-start.4 = (f32[448,1,512]{2,1,0:T(1,128)S(1)}, f32[448,1,512]{2,1,0:T(1,128)}, u32[]{:S(2)}) copy-start(f32[448,1,512]{2,1,0:T(1,128)} %param.8) | copy-start | bytes 2752516

commit v2 on v1

v2 whole, which is shorter than its diff:
```python
import jax
import jax.numpy as jnp
from jax import lax
from jax.experimental import pallas as pl
from jax.experimental.pallas import tpu as pltpu
from jax.sharding import PartitionSpec as P

STEP = 10
BF16 = jnp.bfloat16
F32 = jnp.float32
MESH = pl.DeviceIdType.MESH


def kernel(
    tokens,
    a_hbm,
    labels_hbm,
    w_hbm,
    grad_ref,
    factor_ref,
    loss_ref,
    a_v,
    labels_ref,
    w32,
    wbuf,
    arx,
    slopes,
    acc,
    part,
    dbuf,
    xsend,
    xrecv,
    slots1,
    slots2,
    ld_sem,
    ws_sem,
    wr_sem,
    ds_sem,
    dr_sem,
    as_sem,
    ar_sem,
    ss_sem,
    sr_sem,
    es_sem,
    er_sem,
    xs_sem,
    xr_sem,
    p1s,
    p1r,
    p2s,
    p2r,
    mid1,
    mid2,
):
    tok = a_v.shape[0]
    width = wbuf.shape[1]
    rows = wbuf.shape[0] // 16
    half = rows // 2
    chip = 2 * rows
    d = lax.axis_index("dp")
    lay = lax.axis_index("layer")
    x = d // 8
    y = (d // 2) % 4
    c = d % 2

    def dp_of(dx, dy, dc=0):
        return ((x + dx) % 2) * 8 + ((y + dy) % 4) * 2 + (c + dc) % 2

    load_a = pltpu.make_async_copy(a_hbm, a_v, ld_sem.at[0])
    load_w = pltpu.make_async_copy(w_hbm, w32, ld_sem.at[1])
    load_labels = pltpu.make_async_copy(labels_hbm, labels_ref, ld_sem.at[2])
    load_w.start()
    load_a.start()
    load_labels.start()

    away = (lay + 4) % 8
    z_next, z_last = (lay // 4 * 4 + (lay + k) % 4 for k in (1, 3))
    near = [
        {"dp": dp_of(1, 0)},
        {"dp": dp_of(1, 0), "layer": away},
        {"dp": dp_of(0, 1)},
        {"dp": dp_of(0, 3)},
        {"dp": dp_of(0, 0, 1)},
        {"layer": z_next},
        {"layer": z_last},
    ]
    barrier = pltpu.get_barrier_semaphore()
    for who in near:
        pl.semaphore_signal(barrier, inc=1, device_id=who, device_id_type=MESH)

    with jax.named_scope("start"):
        load_w.wait()
        own = pl.multiple_of(d * rows, 64)

        def convert(g, carry):
            for j in range(4):
                v = w32[pl.ds(g * 64 + j, 16, stride=4), :]
                wbuf[pl.ds(pl.multiple_of(own + g * 16, 16), 16), j * 128 : (j + 1) * 128] = v.astype(BF16)
            return carry

        lax.fori_loop(0, rows // 16, convert, 0)
        with jax.named_scope("barrier"):
            pl.semaphore_wait(barrier, len(near))

    sent = []

    def send(src, dst, ssem, rsem, dp):
        cp = pltpu.make_async_remote_copy(
            src_ref=src, dst_ref=dst, send_sem=ssem, recv_sem=rsem,
            device_id={"dp": dp}, device_id_type=MESH,
        )
        cp.start()
        sent.append(cp)
        return cp

    def w_rows(dx, dy, dc, h):
        start = pl.multiple_of(dp_of(dx, dy, dc) * rows + h * half, 32)
        return wbuf.at[pl.ds(start, half), :]

    wcount = [0]

    def w_send(dx, dy, h, tx, ty):
        ref = w_rows(dx, dy, 0, h)
        k = ((dx - tx) % 2) * 4 + (dy - ty) % 4
        i = wcount[0]
        wcount[0] += 1
        send(ref, ref, ws_sem.at[i], wr_sem.at[k, h], dp_of(tx, ty))

    def w_pass(dx, dy, h):
        ref = w_rows(dx, dy, 0, h)
        k = dx * 4 + dy
        send(ref, ref, ds_sem.at[k, h], dr_sem.at[k, h], dp_of(0, 0, 1))

    def w_wait(dx, dy, h):
        ref = w_rows(dx, dy, 0, h)
        pltpu.make_async_remote_copy(
            src_ref=ref, dst_ref=ref, send_sem=ws_sem.at[0], recv_sem=wr_sem.at[dx * 4 + dy, h],
            device_id={"dp": dp_of(0, 0, 1)}, device_id_type=MESH,
        ).wait_recv()

    def d_wait(dx, dy, h):
        ref = w_rows(dx, dy, 1, h)
        pltpu.make_async_remote_copy(
            src_ref=ref, dst_ref=ref, send_sem=ws_sem.at[0], recv_sem=dr_sem.at[dx * 4 + dy, h],
            device_id={"dp": dp_of(0, 0, 1)}, device_id_type=MESH,
        ).wait_recv()

    def a_cols(dx, dy):
        return pl.multiple_of((((x + dx) % 2) * 4 + (y + dy) % 4) * chip, 128)

    cuts = (pl.ds(0, 256), pl.ds(256, chip - 256))

    def a_send(e, dx, dy, part):
        cut = cuts[part]
        send(
            a_hbm.at[:, pl.ds(pl.multiple_of(a_cols(dx, dy) + cut.start, 128), cut.size)],
            arx.at[dy - 1, e, :, cut],
            as_sem.at[dy - 1, e, part], ar_sem.at[dy - 1, e, part], dp_of(0, dy),
        )

    def a_wait(e, dy):
        for part, cut in enumerate(cuts):
            ref = arx.at[dy - 1, e, :, cut]
            pltpu.make_async_remote_copy(
                src_ref=ref, dst_ref=ref,
                send_sem=as_sem.at[dy - 1, e, part], recv_sem=ar_sem.at[dy - 1, e, part],
                device_id={"dp": dp_of(0, dy)}, device_id_type=MESH,
            ).wait_recv()

    acc[...] = jnp.zeros_like(acc)

    def logits_of(dx, dy):
        cols = a_cols(dx, dy)
        for h in range(2):
            d_wait(dx, dy, h)

        def step(n, carry):
            lanes = pl.ds(pl.multiple_of(n * 256, 256), 256)
            acc[:, lanes] += jnp.dot(
                a_v[:, pl.ds(cols, chip)], wbuf[pl.ds(cols, chip), lanes],
                preferred_element_type=F32,
            )
            return carry

        lax.fori_loop(0, width // 256, step, 0)

    for who in near[-2:]:
        pl.semaphore_signal(mid1, inc=1, device_id=who, device_id_type=MESH)
    with jax.named_scope("own"):
        w_send(0, 0, 0, 1, 0)
        w_send(0, 0, 0, 0, 1)
        w_send(0, 0, 1, 0, 3)
        w_send(0, 0, 1, 1, 0)
        w_send(0, 0, 1, 0, 1)
        w_send(0, 0, 0, 0, 3)
        w_pass(0, 0, 0)
        w_pass(0, 0, 1)
        load_a.wait()
        load_labels.wait()

    with jax.named_scope("relay1"):
        w_wait(0, 3, 0)
        w_send(0, 3, 0, 0, 1)
        w_send(0, 3, 0, 1, 0)
        w_pass(0, 3, 0)
        w_wait(0, 1, 1)
        w_send(0, 1, 1, 0, 3)
        w_send(0, 1, 1, 1, 0)
        w_pass(0, 1, 1)
        w_wait(1, 0, 0)
        w_send(1, 0, 0, 0, 3)
        w_pass(1, 0, 0)
        w_wait(1, 0, 1)
        w_send(1, 0, 1, 0, 1)
        w_pass(1, 0, 1)

    for dy in (2, 1, 3):
        for cut in range(2):
            a_send(0, 1, dy, cut)
    with jax.named_scope("log1"):
        logits_of(0, 0)
        w_wait(0, 3, 1)
        w_pass(0, 3, 1)
        w_wait(0, 1, 0)
        w_pass(0, 1, 0)
        logits_of(1, 0)

    with jax.named_scope("log2"):
        w_wait(0, 2, 0)
        w_send(0, 2, 0, 1, 0)
        w_pass(0, 2, 0)
        w_wait(0, 2, 1)
        w_send(0, 2, 1, 1, 0)
        w_pass(0, 2, 1)
        logits_of(0, 3)
        logits_of(0, 1)
        logits_of(0, 2)

    with jax.named_scope("log3"):
        w_wait(1, 3, 1)
        w_pass(1, 3, 1)
        w_wait(1, 1, 0)
        w_pass(1, 1, 0)
        w_wait(1, 3, 0)
        w_pass(1, 3, 0)
        w_wait(1, 1, 1)
        w_pass(1, 1, 1)
        logits_of(1, 3)
        logits_of(1, 1)

    with jax.named_scope("log4"):
        w_wait(1, 2, 0)
        w_pass(1, 2, 0)
        w_wait(1, 2, 1)
        w_pass(1, 2, 1)
        logits_of(1, 2)

    with jax.named_scope("softmax"):
        classes = lax.broadcasted_iota(jnp.int32, (128, width), 1)
        loss_lanes = jnp.zeros((1, 128), F32)
        for t in range(tok // 128):
            lab = jnp.broadcast_to(labels_ref[t : t + 1, :], (128, 128)).T
            lab = jnp.concatenate([lab] * (width // 128), axis=1)
            logits = acc[t * 128 : (t + 1) * 128, :]
            top = jnp.max(logits, axis=1, keepdims=True)
            exps = jnp.exp(logits - top)
            denom = jnp.sum(exps, axis=1, keepdims=True)
            onehot = (lab == classes).astype(F32)
            picked = jnp.sum(logits * onehot, axis=1, keepdims=True)
            probs = exps / denom
            slopes[0, t * 128 : (t + 1) * 128, :] = ((probs - onehot) / tokens).astype(BF16)
            term = top + jnp.log(denom) - picked
            loss_lanes += jnp.sum(jnp.broadcast_to(term, (128, 128)), axis=0, keepdims=True)

    def slope_send(src, dy, rows, i, k):
        send(
            slopes.at[src, rows, :], slopes.at[(src + dy) % 4, rows, :],
            ss_sem.at[i], sr_sem.at[k], dp_of(0, dy),
        )

    def slope_wait(slot, rows, k):
        pltpu.make_async_remote_copy(
            src_ref=slopes.at[slot, rows, :], dst_ref=slopes.at[slot, rows, :],
            send_sem=ss_sem.at[0], recv_sem=sr_sem.at[k],
            device_id={"dp": dp_of(0, 1)}, device_id_type=MESH,
        ).wait_recv()

    every, upper, lower = pl.ds(0, tok), pl.ds(0, tok // 2), pl.ds(tok // 2, tok // 2)
    slope_send(0, 1, every, 0, 0)
    slope_send(0, 3, every, 1, 1)
    for dy in (1, 3):
        a_send(1, 0, dy, 0)
    pl.semaphore_wait(mid1, 2)
    pl.semaphore_signal(mid2, inc=1, device_id={"layer": away}, device_id_type=MESH)

    def outer(left, right):
        return lax.dot_general(
            left, right, (((0,), (0,)), ((), ())), preferred_element_type=F32
        )

    def accumulate(e, dx, dy, first, start, count):
        at = pl.multiple_of(start, 128)
        if dy == 0:
            left = a_v[:, pl.ds(pl.multiple_of(a_cols(dx, 0) + at, 128), count)]
        else:
            left = arx[dy - 1, e, :, pl.ds(at, count)]
        here = outer(left, slopes[dy])
        if first:
            part[e, pl.ds(at, count), :] = here
        else:
            part[e, pl.ds(at, count), :] += here

    mine = pl.multiple_of(c * rows, 64)
    other = pl.multiple_of((1 - c) * rows, 64)
    big = (1 - c) * 384
    small = c * 512

    def exchange(e, h):
        return send(
            part.at[e, pl.ds(pl.multiple_of(other + h * half, 32), half), :],
            dbuf.at[e, pl.ds(h * half, half), :],
            es_sem.at[e, h], er_sem.at[e, h], dp_of(0, 0, 1),
        )

    accumulate(0, 1, 0, True, big, 512)
    with jax.named_scope("slope1"):
        slope_wait(1, every, 0)
        slope_send(1, 1, upper, 2, 2)
        slope_wait(3, every, 1)
        slope_send(3, 3, lower, 3, 3)
        a_send(1, 0, 2, 0)
        for dy in (1, 3, 2):
            a_send(1, 0, dy, 1)
    with jax.named_scope("gradx1"):
        for dy in (1, 3):
            a_wait(0, dy)
            accumulate(0, 1, dy, False, big, 512)
    with jax.named_scope("slope2"):
        slope_wait(2, upper, 2)
        slope_wait(2, lower, 3)
    with jax.named_scope("gradx1b"):
        a_wait(0, 2)
        accumulate(0, 1, 2, False, big, 512)

    with jax.named_scope("gradx2"):
        swaps = [exchange(0, h) for h in range(2)]
        for dy in (0, 1, 3, 2):
            accumulate(0, 1, dy, dy == 0, small, 384)
        xs = []
        for h in range(2):
            swaps[h].wait_recv()
            piece = pl.ds(h * half, half)
            xsend[piece, :] = part[0, pl.ds(pl.multiple_of(mine + h * half, 32), half), :] + dbuf[0, piece, :]
            xs.append(send(xsend.at[piece, :], xrecv.at[piece, :], xs_sem.at[h], xr_sem.at[h], dp_of(1, 0)))

    with jax.named_scope("grado1"):
        for dy in (0, 2, 1, 3):
            if dy:
                a_wait(1, dy)
            accumulate(1, 0, dy, dy == 0, big, 512)
            if dy != 3:
                accumulate(1, 0, dy, dy == 0, small, 384)

    with jax.named_scope("grado2"):
        swaps = [exchange(1, h) for h in range(2)]
        accumulate(1, 0, 3, False, small, 384)
        for h in range(2):
            swaps[h].wait_recv()

    with jax.named_scope("xwait"):
        for h in range(2):
            xs[h].wait_recv()

    def finish(g, carry):
        r = pl.multiple_of(g * 8, 8)
        m = pl.multiple_of(mine + g * 8, 8)
        for j in range(4):
            lanes = slice(j * 128, (j + 1) * 128)
            v = part[1, pl.ds(m, 8), lanes] + dbuf[1, pl.ds(r, 8), lanes] + xrecv[pl.ds(r, 8), lanes]
            grad_ref[pl.ds(g * 32 + j, 8, stride=4), :] = v
            carry = carry + v * v
        return carry

    with jax.named_scope("fin"):
        square = lax.fori_loop(0, rows // 8, finish, jnp.zeros((8, 128), F32))
        tile = jnp.concatenate(
            [jnp.sum(square, axis=0, keepdims=True), loss_lanes, jnp.zeros((6, 128), F32)], axis=0
        )

    with jax.named_scope("red1"):
        slots1[d] = tile
        first = []
        for k in range(1, 16):
            cp = pltpu.make_async_remote_copy(
                src_ref=slots1.at[d], dst_ref=slots1.at[d], send_sem=p1s.at[k - 1],
                recv_sem=p1r.at[k - 1], device_id={"dp": (d + k) % 16}, device_id_type=MESH,
            )
            cp.start()
            first.append(cp)
        for cp in first:
            cp.wait()

    with jax.named_scope("red2"):
        pl.semaphore_wait(mid2, 1)
        slots2[lay] = jnp.sum(slots1[...], axis=0)
        second = []
        for k in range(1, 8):
            cp = pltpu.make_async_remote_copy(
                src_ref=slots2.at[lay], dst_ref=slots2.at[lay], send_sem=p2s.at[k - 1],
                recv_sem=p2r.at[k - 1], device_id={"layer": (lay + k) % 8}, device_id_type=MESH,
            )
            cp.start()
            second.append(cp)
        for cp in second:
            cp.wait()

    sums = jnp.sum(slots2[...], axis=0)
    square = jnp.broadcast_to(jnp.sum(sums[0:1, :], axis=1, keepdims=True), (1, 128))
    factor_ref[...] = jnp.minimum(1.0, 0.25 / jnp.sqrt(square + 1e-12))
    loss_ref[...] = sums[1:2, :] / (tokens * 8)
    for cp in sent:
        cp.wait_send()


def shards(activations, labels, weights, first_moment, second_moment):
    tok = activations.shape[0]
    depth = activations.shape[2]
    rows, _, width = weights.shape
    tokens = tok * lax.axis_size("dp")
    dma = pltpu.SemaphoreType.DMA
    vmem = pltpu.VMEM
    lines = rows * width // 128
    anywhere = pl.BlockSpec(memory_space=pltpu.MemorySpace.HBM)
    inside = pl.BlockSpec(memory_space=pltpu.VMEM)

    def body(*refs):
        kernel(tokens, *refs)

    grad, factor, loss = pl.pallas_call(
        body,
        out_shape=(
            jax.ShapeDtypeStruct((lines, 128), F32),
            jax.ShapeDtypeStruct((1, 128), F32),
            jax.ShapeDtypeStruct((1, 128), F32),
        ),
        in_specs=[anywhere, anywhere, anywhere],
        out_specs=(inside, inside, inside),
        scratch_shapes=[
            vmem((tok, depth), BF16),
            vmem((tok // 128, 128), jnp.int32),
            vmem((lines, 128), F32),
            vmem((depth, width), BF16),
            vmem((3, 2, tok, 2 * rows), BF16),
            vmem((4, tok, width), BF16),
            vmem((tok, width), F32),
            vmem((2, 2 * rows, width), F32),
            vmem((2, rows, width), F32),
            vmem((rows, width), F32),
            vmem((rows, width), F32),
            vmem((16, 8, 128), F32),
            vmem((8, 8, 128), F32),
            dma((3,)),
            dma((14,)),
            dma((8, 2)),
            dma((8, 2)),
            dma((8, 2)),
            dma((3, 2, 2)),
            dma((3, 2, 2)),
            dma((4,)),
            dma((4,)),
            dma((2, 2)),
            dma((2, 2)),
            dma((2,)),
            dma((2,)),
            dma((15,)),
            dma((15,)),
            dma((7,)),
            dma((7,)),
            pltpu.SemaphoreType.REGULAR,
            pltpu.SemaphoreType.REGULAR,
        ],
        compiler_params=pltpu.CompilerParams(
            collective_id=0, has_side_effects=True, vmem_limit_bytes=48 << 20
        ),
        name="probe_step",
    )(
        *(
            pltpu.with_memory_space_constraint(v, pltpu.MemorySpace.HBM)
            for v in (
                activations.reshape(tok, depth),
                labels.reshape(tok // 128, 128),
                weights.reshape(lines, 128),
            )
        )
    )
    held = [v.reshape(lines, 128) for v in (weights, first_moment, second_moment)]
    grad, weights, first_moment, second_moment = lax.optimization_barrier((grad, *held))
    clipped = factor * grad
    new_first = 0.9 * first_moment + 0.1 * clipped
    new_second = 0.999 * second_moment + 0.001 * clipped * clipped
    new_weights = weights - 0.001 * (new_first / (1.0 - 0.9**STEP)) / (
        jnp.sqrt(new_second / (1.0 - 0.999**STEP)) + 1e-08
    )
    outs = (v.reshape(rows, 1, width) for v in (new_weights, new_first, new_second))
    return (*outs, loss[0, 0])


def solution(mesh):
    rows = P("dp", "layer", None)
    return jax.shard_map(
        shards,
        mesh=mesh,
        in_specs=(rows, P("dp"), rows, rows, rows),
        out_specs=(rows, rows, rows, P()),
        check_vma=False,
    )
```

time: 121 us -> 101 us (0.83)
  Pallas kernels: 104 us -> 97.1 us
  other arithmetic: 8.44 us -> 1.96 us
  local copies, waits for them, and re-layouts: 4.41 us -> 0.01 us
  between operations: 3.15 us -> 1.85 us
    pallas_call x1, Pallas kernels: 104 us -> 97.1 us  [shards(): pl.pallas_call(body, out_shape=(jax.ShapeDtypeStruct((lines, 128), F32),...]
    sub x1, other arithmetic: 7.78 us -> 1.96 us  [shards(): weights - 0.001 * (new_first / (1.0 - 0.9 ** STEP)) / (jnp.sqrt(new_secon...]
    unnamed x10 -> x6, local copies, waits for them, and re-layouts: 3.9 us -> 0.01 us
where the time goes in v2:
time: 101 us
  Pallas kernels  97.1 us (96%)
  other arithmetic  1.96 us (2%)
  between operations  1.85 us (2%)
    pallas_call x1, Pallas kernels, shards(): pl.pallas_call(body, out_shape=(jax.ShapeDtypeStruct((lines, 128), F32),...  97.1 us

profile of v2, /device:TPU:1, one launch (start us, length us, event | category | flops | bytes accessed | tf_op | source)
XLA Modules:
  0.0 101.0 jit_solution(6709165058632313349)
XLA Ops:
  0.6 0.0 copy-start.2
  0.6 0.0 copy-start.1
  0.7 0.0 copy-start
  0.7 97.1 %probe_step.1 = (f32[1792,128]{1,0:T(8,128)S(1)}, f32[1,128]{1,0:T(1,128)S(1)}, f32[1,128]{1,0:T(1,128)S(1)}) custom-call(bf16[256,7168]{1,0:T(8,128)(2,1)} %bitcast.15, s32[2,128]{1,0:T(2,128)} %bitcast.21, f32[1792,128]{1,0:T(8,128)} %bitcast.13), custom_call_target="tpu_custom_call" | custom-call | tf_op jit(solution)/shard_map/probe_step/pallas_call | solution.py:439
  97.8 0.0 copy-done.2
  97.8 0.0 copy-done.1
  97.8 0.0 copy-done
  97.8 2.0 %divide_subtract_fusion = (f32[1792,128]{1,0:T(8,128)}, f32[1792,128]{1,0:T(8,128)}, f32[1792,128]{1,0:T(8,128)}) fusion(f32[1792,128]{1,0:T(8,128)S(1)} %bitcast.14, f32[1792,128]{1,0:T(8,128)S(1)} %get-tuple-element.15, f32[128]{0:T(128)S(1)} %bitcast.11, f32[1792,128]{1,0:T(8,128)S(1)} %bitcast.16, f32[1792,128]{1,0:T(8,128)S(1)} %bitcast.17), kind=kLoop, calls=%fused_computation.2 | loop fusion | flops 2981888 | bytes 6423040 | tf_op jit(solution)/shard_map/sub | solution.py:501
Async XLA Ops:
  0.6 97.2 %copy-start.2 = (f32[448,1,512]{2,1,0:T(1,128)S(1)}, f32[448,1,512]{2,1,0:T(1,128)}, u32[]{:S(2)}) copy-start(f32[448,1,512]{2,1,0:T(1,128)} %param.9) | copy-start | bytes 2752516
  0.6 97.2 %copy-start.1 = (f32[448,1,512]{2,1,0:T(1,128)S(1)}, f32[448,1,512]{2,1,0:T(1,128)}, u32[]{:S(2)}) copy-start(f32[448,1,512]{2,1,0:T(1,128)} %param.8) | copy-start | bytes 2752516
  0.7 97.2 %copy-start = (f32[448,1,512]{2,1,0:T(1,128)S(1)}, f32[448,1,512]{2,1,0:T(1,128)}, u32[]{:S(2)}) copy-start(f32[448,1,512]{2,1,0:T(1,128)} %param.7) | copy-start | bytes 2752516

commit v3 on v2

--- a/solution.py
+++ b/solution.py
@@ -148,24 +148,26 @@
     def a_cols(dx, dy):
         return pl.multiple_of((((x + dx) % 2) * 4 + (y + dy) % 4) * chip, 128)
 
-    cuts = (pl.ds(0, 256), pl.ds(256, chip - 256))
-
-    def a_send(e, dx, dy, part):
-        cut = cuts[part]
+    cuts = ((0, 256), (640, 256), (256, 128), (384, 128), (512, 128))
+
+    def a_send(e, dx, dy, k):
+        start, size = cuts[k]
         send(
-            a_hbm.at[:, pl.ds(pl.multiple_of(a_cols(dx, dy) + cut.start, 128), cut.size)],
-            arx.at[dy - 1, e, :, cut],
-            as_sem.at[dy - 1, e, part], ar_sem.at[dy - 1, e, part], dp_of(0, dy),
-        )
-
-    def a_wait(e, dy):
-        for part, cut in enumerate(cuts):
-            ref = arx.at[dy - 1, e, :, cut]
+            a_hbm.at[:, pl.ds(pl.multiple_of(a_cols(dx, dy) + start, 128), size)],
+            arx.at[dy - 1, e, :, pl.ds(start, size)],
+            as_sem.at[dy - 1, e, k], ar_sem.at[dy - 1, e, k], dp_of(0, dy),
+        )
+
+    def a_wait(e, dy, which):
+        for k in which:
+            ref = arx.at[dy - 1, e, :, pl.ds(*cuts[k])]
             pltpu.make_async_remote_copy(
                 src_ref=ref, dst_ref=ref,
-                send_sem=as_sem.at[dy - 1, e, part], recv_sem=ar_sem.at[dy - 1, e, part],
+                send_sem=as_sem.at[dy - 1, e, k], recv_sem=ar_sem.at[dy - 1, e, k],
                 device_id={"dp": dp_of(0, dy)}, device_id_type=MESH,
             ).wait_recv()
+
+    ends, middle = (0, 1), (2, 3, 4)
 
     acc[...] = jnp.zeros_like(acc)
 
@@ -214,9 +216,6 @@
         w_send(1, 0, 1, 0, 1)
         w_pass(1, 0, 1)
 
-    for dy in (2, 1, 3):
-        for cut in range(2):
-            a_send(0, 1, dy, cut)
     with jax.named_scope("log1"):
         logits_of(0, 0)
         w_wait(0, 3, 1)
@@ -236,6 +235,9 @@
         logits_of(0, 1)
         logits_of(0, 2)
 
+    for k in (0, 1, 2):
+        for dy in (2, 1, 3):
+            a_send(0, 1, dy, k)
     with jax.named_scope("log3"):
         w_wait(1, 3, 1)
         w_pass(1, 3, 1)
@@ -288,8 +290,7 @@
     every, upper, lower = pl.ds(0, tok), pl.ds(0, tok // 2), pl.ds(tok // 2, tok // 2)
     slope_send(0, 1, every, 0, 0)
     slope_send(0, 3, every, 1, 1)
-    for dy in (1, 3):
-        a_send(1, 0, dy, 0)
+    left_here = [sent.pop(), sent.pop()]
     pl.semaphore_wait(mid1, 2)
     pl.semaphore_signal(mid2, inc=1, device_id={"layer": away}, device_id_type=MESH)
 
@@ -298,123 +299,156 @@
             left, right, (((0,), (0,)), ((), ())), preferred_element_type=F32
         )
 
-    def accumulate(e, dx, dy, first, start, count):
-        at = pl.multiple_of(start, 128)
+    def accumulate(e, dy, start, count):
+        at = start if isinstance(start, int) else pl.multiple_of(start, 128)
         if dy == 0:
-            left = a_v[:, pl.ds(pl.multiple_of(a_cols(dx, 0) + at, 128), count)]
+            left = a_v[:, pl.ds(pl.multiple_of(a_cols(1 - e, 0) + at, 128), count)]
         else:
             left = arx[dy - 1, e, :, pl.ds(at, count)]
         here = outer(left, slopes[dy])
-        if first:
+        if dy == 0:
             part[e, pl.ds(at, count), :] = here
         else:
             part[e, pl.ds(at, count), :] += here
 
-    mine = pl.multiple_of(c * rows, 64)
-    other = pl.multiple_of((1 - c) * rows, 64)
-    big = (1 - c) * 384
-    small = c * 512
-
-    def exchange(e, h):
+    groups = (
+        (lambda k: k * 640, lambda k: k * 192, 256),
+        (lambda k: 256 + k * 192, lambda k: (1 - k) * 256, 192),
+    )
+
+    def in_part(g, k):
+        return pl.ds(pl.multiple_of(groups[g][0](k), 64), groups[g][2])
+
+    def in_block(g, k):
+        return pl.ds(pl.multiple_of(groups[g][1](k), 64), groups[g][2])
+
+    def exchange(e, g):
         return send(
-            part.at[e, pl.ds(pl.multiple_of(other + h * half, 32), half), :],
-            dbuf.at[e, pl.ds(h * half, half), :],
-            es_sem.at[e, h], er_sem.at[e, h], dp_of(0, 0, 1),
-        )
-
-    accumulate(0, 1, 0, True, big, 512)
+            part.at[e, in_part(g, 1 - c), :], dbuf.at[e, in_block(g, 1 - c), :],
+            es_sem.at[e, g], er_sem.at[e, g], dp_of(0, 0, 1),
+        )
+
+    def swap_wait(e, g):
+        ref = dbuf.at[e, in_block(g, c), :]
+        pltpu.make_async_remote_copy(
+            src_ref=ref, dst_ref=ref, send_sem=es_sem.at[e, g], recv_sem=er_sem.at[e, g],
+            device_id={"dp": dp_of(0, 0, 1)}, device_id_type=MESH,
+        ).wait_recv()
+
+    def x_send(g):
+        swap_wait(0, g)
+        block = in_block(g, c)
+        xsend[block, :] = part[0, in_part(g, c), :] + dbuf[0, block, :]
+        return send(
+            xsend.at[block, :], xrecv.at[block, :], xs_sem.at[g], xr_sem.at[g], dp_of(1, 0)
+        )
+
+    def finish(group, carry):
+        swap_wait(1, group)
+        size = groups[group][2]
+        theirs, block = groups[group][0](c), groups[group][1](c)
+
+        def step(g, carry):
+            r = pl.multiple_of(block + g * 8, 8)
+            m = pl.multiple_of(theirs + g * 8, 8)
+            for j in range(4):
+                lanes = slice(j * 128, (j + 1) * 128)
+                v = part[1, pl.ds(m, 8), lanes] + dbuf[1, pl.ds(r, 8), lanes] + xrecv[pl.ds(r, 8), lanes]
+                grad_ref[pl.ds(r * 4 + j, 8, stride=4), :] = v
+                carry = carry + v * v
+            return carry
+
+        return lax.fori_loop(0, size // 8, step, carry)
+
+    with jax.named_scope("grad0"):
+        for e in range(2):
+            accumulate(e, 0, 0, 512)
+            accumulate(e, 0, 512, 384)
+    with jax.named_scope("slopesent"):
+        for cp in left_here:
+            cp.wait_send()
+        for dy in (2, 1, 3):
+            a_send(0, 1, dy, 3)
     with jax.named_scope("slope1"):
         slope_wait(1, every, 0)
         slope_send(1, 1, upper, 2, 2)
         slope_wait(3, every, 1)
         slope_send(3, 3, lower, 3, 3)
-        a_send(1, 0, 2, 0)
-        for dy in (1, 3, 2):
-            a_send(1, 0, dy, 1)
+        for dy in (2, 1, 3):
+            a_send(0, 1, dy, 4)
+    yours, mine = (1 - c) * 640, c * 640
     with jax.named_scope("gradx1"):
         for dy in (1, 3):
-            a_wait(0, dy)
-            accumulate(0, 1, dy, False, big, 512)
+            a_wait(0, dy, ends)
+            accumulate(0, dy, yours, 256)
+            accumulate(0, dy, mine, 256)
     with jax.named_scope("slope2"):
         slope_wait(2, upper, 2)
         slope_wait(2, lower, 3)
-    with jax.named_scope("gradx1b"):
-        a_wait(0, 2)
-        accumulate(0, 1, 2, False, big, 512)
-
+    for which in (ends, middle):
+        for k in which:
+            for dy in (2, 1, 3):
+                a_send(1, 0, dy, k)
     with jax.named_scope("gradx2"):
-        swaps = [exchange(0, h) for h in range(2)]
-        for dy in (0, 1, 3, 2):
-            accumulate(0, 1, dy, dy == 0, small, 384)
-        xs = []
-        for h in range(2):
-            swaps[h].wait_recv()
-            piece = pl.ds(h * half, half)
-            xsend[piece, :] = part[0, pl.ds(pl.multiple_of(mine + h * half, 32), half), :] + dbuf[0, piece, :]
-            xs.append(send(xsend.at[piece, :], xrecv.at[piece, :], xs_sem.at[h], xr_sem.at[h], dp_of(1, 0)))
-
+        a_wait(0, 2, ends)
+        accumulate(0, 2, yours, 256)
+        exchange(0, 0)
+        accumulate(0, 2, mine, 256)
+        pl.semaphore_wait(mid2, 1)
+        xs = [x_send(0)]
+    with jax.named_scope("gradx3"):
+        for dy in (1, 3, 2):
+            a_wait(0, dy, middle)
+            accumulate(0, dy, 256, 384)
+        exchange(0, 1)
+        xs.append(x_send(1))
     with jax.named_scope("grado1"):
-        for dy in (0, 2, 1, 3):
-            if dy:
-                a_wait(1, dy)
-            accumulate(1, 0, dy, dy == 0, big, 512)
-            if dy != 3:
-                accumulate(1, 0, dy, dy == 0, small, 384)
-
+        for dy in (1, 3, 2):
+            a_wait(1, dy, ends)
+            accumulate(1, dy, yours, 256)
+            accumulate(1, dy, mine, 256)
+        exchange(1, 0)
+    with jax.named_scope("fin1"):
+        xs[0].wait_recv()
+        square = finish(0, jnp.zeros((8, 128), F32))
     with jax.named_scope("grado2"):
-        swaps = [exchange(1, h) for h in range(2)]
-        accumulate(1, 0, 3, False, small, 384)
-        for h in range(2):
-            swaps[h].wait_recv()
-
+        for dy in (1, 3, 2):
+            a_wait(1, dy, middle)
+            accumulate(1, dy, 256, 384)
+        exchange(1, 1)
     with jax.named_scope("xwait"):
-        for h in range(2):
-            xs[h].wait_recv()
-
-    def finish(g, carry):
-        r = pl.multiple_of(g * 8, 8)
-        m = pl.multiple_of(mine + g * 8, 8)
-        for j in range(4):
-            lanes = slice(j * 128, (j + 1) * 128)
-            v = part[1, pl.ds(m, 8), lanes] + dbuf[1, pl.ds(r, 8), lanes] + xrecv[pl.ds(r, 8), lanes]
-            grad_ref[pl.ds(g * 32 + j, 8, stride=4), :] = v
-            carry = carry + v * v
-        return carry
-
-    with jax.named_scope("fin"):
-        square = lax.fori_loop(0, rows // 8, finish, jnp.zeros((8, 128), F32))
+        xs[1].wait_recv()
+    with jax.named_scope("fin2"):
+        square = finish(1, square)
         tile = jnp.concatenate(
             [jnp.sum(square, axis=0, keepdims=True), loss_lanes, jnp.zeros((6, 128), F32)], axis=0
         )
 
-    with jax.named_scope("red1"):
-        slots1[d] = tile
-        first = []
-        for k in range(1, 16):
+    def spread(slots, here, index, peers, ssem, rsem):
+        slots[index] = here
+        copies = []
+        for k, who in enumerate(peers):
             cp = pltpu.make_async_remote_copy(
-                src_ref=slots1.at[d], dst_ref=slots1.at[d], send_sem=p1s.at[k - 1],
-                recv_sem=p1r.at[k - 1], device_id={"dp": (d + k) % 16}, device_id_type=MESH,
+                src_ref=slots.at[index], dst_ref=slots.at[index], send_sem=ssem.at[k],
+                recv_sem=rsem.at[k], device_id=who, device_id_type=MESH,
             )
             cp.start()
-            first.append(cp)
-        for cp in first:
+            copies.append(cp)
+        for cp in copies:
             cp.wait()
-
+        return jnp.sum(slots[...], axis=0)
+
+    m = y * 2 + c
+    n = x * 8 + lay
+    with jax.named_scope("red1"):
+        tile = spread(
+            slots1, tile, m, [{"dp": x * 8 + (m + k) % 8} for k in range(1, 8)], p1s, p1r
+        )
     with jax.named_scope("red2"):
-        pl.semaphore_wait(mid2, 1)
-        slots2[lay] = jnp.sum(slots1[...], axis=0)
-        second = []
-        for k in range(1, 8):
-            cp = pltpu.make_async_remote_copy(
-                src_ref=slots2.at[lay], dst_ref=slots2.at[lay], send_sem=p2s.at[k - 1],
-                recv_sem=p2r.at[k - 1], device_id={"layer": (lay + k) % 8}, device_id_type=MESH,
-            )
-            cp.start()
-            second.append(cp)
-        for cp in second:
-            cp.wait()
-
-    sums = jnp.sum(slots2[...], axis=0)
+        others = [(n + k) % 16 for k in range(1, 16)]
+        sums = spread(
+            slots2, tile, n, [{"dp": o // 8 * 8 + m, "layer": o % 8} for o in others], p2s, p2r
+        )
     square = jnp.broadcast_to(jnp.sum(sums[0:1, :], axis=1, keepdims=True), (1, 128))
     factor_ref[...] = jnp.minimum(1.0, 0.25 / jnp.sqrt(square + 1e-12))
     loss_ref[...] = sums[1:2, :] / (tokens * 8)
@@ -457,25 +491,25 @@
             vmem((2, rows, width), F32),
             vmem((rows, width), F32),
             vmem((rows, width), F32),
+            vmem((8, 8, 128), F32),
             vmem((16, 8, 128), F32),
-            vmem((8, 8, 128), F32),
             dma((3,)),
             dma((14,)),
             dma((8, 2)),
             dma((8, 2)),
             dma((8, 2)),
-            dma((3, 2, 2)),
-            dma((3, 2, 2)),
+            dma((3, 2, 5)),
+            dma((3, 2, 5)),
             dma((4,)),
             dma((4,)),
             dma((2, 2)),
             dma((2, 2)),
             dma((2,)),
             dma((2,)),
+            dma((7,)),
+            dma((7,)),
             dma((15,)),
             dma((15,)),
-            dma((7,)),
-            dma((7,)),
             pltpu.SemaphoreType.REGULAR,
             pltpu.SemaphoreType.REGULAR,
         ],

time: 101 us -> 94.7 us (0.938)
  Pallas kernels: 97.1 us -> 90.8 us
    pallas_call x1, Pallas kernels: 97.1 us -> 90.8 us  [shards(): pl.pallas_call(body, out_shape=(jax.ShapeDtypeStruct((lines, 128), F32),...]
where the time goes in v3:
time: 94.7 us; the launch traced here: 94.6 us
  Pallas kernels  90.8 us (96%)
  other arithmetic  1.96 us (2%)
  between operations  1.85 us (2%)
    pallas_call x1, Pallas kernels, shards(): pl.pallas_call(body, out_shape=(jax.ShapeDtypeStruct((lines, 128), F32),...  90.8 us
    sub x1, other arithmetic, shards(): weights - 0.001 * (new_first / (1.0 - 0.9 ** STEP)) / (jnp.sqrt(new_secon...  1.96 us

profile of v3, /device:TPU:1, one launch (start us, length us, event | category | flops | bytes accessed | tf_op | source)
XLA Modules:
  0.0 94.6 jit_solution(17179084742160877762)
XLA Ops:
  0.6 0.0 copy-start.2
  0.6 0.0 copy-start.1
  0.7 0.0 copy-start
  0.7 90.8 %probe_step.1 = (f32[1792,128]{1,0:T(8,128)S(1)}, f32[1,128]{1,0:T(1,128)S(1)}, f32[1,128]{1,0:T(1,128)S(1)}) custom-call(bf16[256,7168]{1,0:T(8,128)(2,1)} %bitcast.15, s32[2,128]{1,0:T(2,128)} %bitcast.21, f32[1792,128]{1,0:T(8,128)} %bitcast.13), custom_call_target="tpu_custom_call" | custom-call | tf_op jit(solution)/shard_map/probe_step/pallas_call | solution.py:473
  91.4 0.0 copy-done.2
  91.5 0.0 copy-done.1
  91.5 0.0 copy-done
  91.5 2.0 %divide_subtract_fusion = (f32[1792,128]{1,0:T(8,128)}, f32[1792,128]{1,0:T(8,128)}, f32[1792,128]{1,0:T(8,128)}) fusion(f32[1792,128]{1,0:T(8,128)S(1)} %bitcast.14, f32[1792,128]{1,0:T(8,128)S(1)} %get-tuple-element.15, f32[128]{0:T(128)S(1)} %bitcast.11, f32[1792,128]{1,0:T(8,128)S(1)} %bitcast.16, f32[1792,128]{1,0:T(8,128)S(1)} %bitcast.17), kind=kLoop, calls=%fused_computation.2 | loop fusion | flops 2981888 | bytes 6423040 | tf_op jit(solution)/shard_map/sub | solution.py:535
Async XLA Ops:
  0.6 90.8 %copy-start.2 = (f32[448,1,512]{2,1,0:T(1,128)S(1)}, f32[448,1,512]{2,1,0:T(1,128)}, u32[]{:S(2)}) copy-start(f32[448,1,512]{2,1,0:T(1,128)} %param.9) | copy-start | bytes 2752516
  0.6 90.8 %copy-start.1 = (f32[448,1,512]{2,1,0:T(1,128)S(1)}, f32[448,1,512]{2,1,0:T(1,128)}, u32[]{:S(2)}) copy-start(f32[448,1,512]{2,1,0:T(1,128)} %param.8) | copy-start | bytes 2752516
  0.7 90.8 %copy-start = (f32[448,1,512]{2,1,0:T(1,128)S(1)}, f32[448,1,512]{2,1,0:T(1,128)}, u32[]{:S(2)}) copy-start(f32[448,1,512]{2,1,0:T(1,128)} %param.7) | copy-start | bytes 2752516

commit v4 on v3

v4 whole, which is shorter than its diff:
```python
import jax
import jax.numpy as jnp
from jax import lax
from jax.experimental import pallas as pl
from jax.experimental.pallas import tpu as pltpu
from jax.sharding import PartitionSpec as P

STEP = 10
BF16 = jnp.bfloat16
F32 = jnp.float32
MESH = pl.DeviceIdType.MESH


def kernel(
    tokens,
    a_hbm,
    labels_hbm,
    w_hbm,
    grad_ref,
    factor_ref,
    loss_ref,
    a_v,
    labels_ref,
    w32,
    wbuf,
    a_far,
    slopes,
    acc,
    part,
    sbuf,
    rbuf,
    sscale,
    rscale,
    slots1,
    slots2,
    ld_sem,
    ws_sem,
    wr_sem,
    ds_sem,
    dr_sem,
    as_sem,
    ar_sem,
    ss_sem,
    sr_sem,
    ms_sem,
    mr_sem,
    p1s,
    p1r,
    p2s,
    p2r,
    mid1,
    mid2,
):
    tok = a_v.shape[0]
    width = wbuf.shape[1]
    rows = wbuf.shape[0] // 16
    quarter = rows // 4
    chip = 2 * rows
    d = lax.axis_index("dp")
    lay = lax.axis_index("layer")
    x = d // 8
    y = (d // 2) % 4
    c = d % 2

    def dp_of(dx, dy, dc=0):
        return ((x + dx) % 2) * 8 + ((y + dy) % 4) * 2 + (c + dc) % 2

    load_a = pltpu.make_async_copy(a_hbm, a_v, ld_sem.at[0])
    load_w = pltpu.make_async_copy(w_hbm, w32, ld_sem.at[1])
    load_labels = pltpu.make_async_copy(labels_hbm, labels_ref, ld_sem.at[2])
    load_w.start()
    load_a.start()
    load_labels.start()

    away = (lay + 4) % 8
    z_next, z_last = (lay // 4 * 4 + (lay + k) % 4 for k in (1, 3))
    near = [
        {"dp": dp_of(1, 0)},
        {"dp": dp_of(1, 0), "layer": away},
        {"dp": dp_of(0, 1)},
        {"dp": dp_of(0, 3)},
        {"dp": dp_of(0, 0, 1)},
        {"layer": z_next},
        {"layer": z_last},
    ]
    barrier = pltpu.get_barrier_semaphore()
    for who in near:
        pl.semaphore_signal(barrier, inc=1, device_id=who, device_id_type=MESH)

    with jax.named_scope("start"):
        load_w.wait()
        own = pl.multiple_of(d * rows, 64)

        def convert(g, carry):
            for j in range(4):
                v = w32[pl.ds(g * 64 + j, 16, stride=4), :]
                wbuf[pl.ds(pl.multiple_of(own + g * 16, 16), 16), j * 128 : (j + 1) * 128] = v.astype(BF16)
            return carry

        lax.fori_loop(0, rows // 16, convert, 0)
        with jax.named_scope("barrier"):
            pl.semaphore_wait(barrier, len(near))

    sent = []

    def copy_of(src, dst, ssem, rsem, dp):
        return pltpu.make_async_remote_copy(
            src_ref=src, dst_ref=dst, send_sem=ssem, recv_sem=rsem,
            device_id={"dp": dp}, device_id_type=MESH,
        )

    def send(*what):
        cp = copy_of(*what)
        cp.start()
        sent.append(cp)

    def arrived(ref, rsem):
        copy_of(ref, ref, ws_sem.at[0], rsem, dp_of(0, 0, 1)).wait_recv()

    def w_rows(dx, dy, dc, q):
        start = pl.multiple_of(dp_of(dx, dy, dc) * rows + q * quarter, 16)
        return wbuf.at[pl.ds(start, quarter), :]

    wcount = [0]

    def w_send(dx, dy, q, *targets):
        ref = w_rows(dx, dy, 0, q)
        for tx, ty in targets:
            k = ((dx - tx) % 2) * 4 + (dy - ty) % 4
            send(ref, ref, ws_sem.at[wcount[0]], wr_sem.at[k, q], dp_of(tx, ty))
            wcount[0] += 1

    def w_pass(dx, dy, q):
        ref = w_rows(dx, dy, 0, q)
        k = dx * 4 + dy
        send(ref, ref, ds_sem.at[k, q], dr_sem.at[k, q], dp_of(0, 0, 1))

    def w_take(dx, dy, q, *targets):
        arrived(w_rows(dx, dy, 0, q), wr_sem.at[dx * 4 + dy, q])
        w_send(dx, dy, q, *targets)
        w_pass(dx, dy, q)

    def chip_cols(dx, dy):
        return pl.multiple_of((((x + dx) % 2) * 4 + (y + dy) % 4) * chip, 128)

    acc[...] = jnp.zeros_like(acc)

    def logits_of(dx, dy):
        cols = chip_cols(dx, dy)
        for q in range(4):
            arrived(w_rows(dx, dy, 1, q), dr_sem.at[dx * 4 + dy, q])

        def step(n, carry):
            lanes = pl.ds(pl.multiple_of(n * 256, 256), 256)
            acc[:, lanes] += jnp.dot(
                a_v[:, pl.ds(cols, chip)], wbuf[pl.ds(cols, chip), lanes],
                preferred_element_type=F32,
            )
            return carry

        lax.fori_loop(0, width // 256, step, 0)

    X, UP, DOWN = (1, 0), (0, 1), (0, 3)
    for who in near[-2:]:
        pl.semaphore_signal(mid1, inc=1, device_id=who, device_id_type=MESH)
    with jax.named_scope("own"):
        for dest, q in (
            (X, 0), (UP, 2), (DOWN, 3), (X, 1), (UP, 3), (DOWN, 2),
            (X, 2), (UP, 0), (DOWN, 1), (X, 3), (UP, 1), (DOWN, 0),
        ):
            w_send(0, 0, q, dest)
        for q in range(4):
            w_pass(0, 0, q)
        for k in range(8):
            start = pl.multiple_of(k * chip + (1 - c) * 384, 128)
            send(
                a_hbm.at[:, pl.ds(start, 512)], a_far.at[k], as_sem.at[k], ar_sem.at[k],
                dp_of(0, 0, 1),
            )
        load_a.wait()
        load_labels.wait()

    with jax.named_scope("relay1"):
        w_take(0, 3, 2, UP, X)
        w_take(0, 1, 3, DOWN, X)
        w_take(0, 3, 3, X)
        w_take(0, 1, 2, X)
        w_take(1, 0, 0, UP, DOWN)
        w_take(1, 0, 1, UP, DOWN)
    with jax.named_scope("relay2"):
        logits_of(0, 0)
        w_take(0, 3, 0, UP)
        w_take(0, 1, 1, DOWN)
        w_take(0, 3, 1)
        w_take(0, 1, 0)
        w_take(1, 0, 2)
        w_take(1, 0, 3)
    with jax.named_scope("relay3"):
        w_take(0, 2, 2, X)
        w_take(0, 2, 3, X)
        logits_of(1, 0)
        logits_of(0, 3)
        logits_of(0, 1)
    with jax.named_scope("relay4"):
        w_take(1, 3, 0, UP)
        w_take(1, 1, 1, DOWN)
        w_take(1, 3, 1)
        w_take(1, 1, 0)
    with jax.named_scope("relay5"):
        for q in (2, 3):
            w_take(1, 3, q)
            w_take(1, 1, q)
        w_take(0, 2, 0)
        w_take(0, 2, 1)
        logits_of(0, 2)
        logits_of(1, 3)
        logits_of(1, 1)
    with jax.named_scope("relay6"):
        for q in range(4):
            w_take(1, 2, q)
        logits_of(1, 2)

    with jax.named_scope("softmax"):
        classes = lax.broadcasted_iota(jnp.int32, (128, width), 1)
        loss_lanes = jnp.zeros((1, 128), F32)
        for t in range(tok // 128):
            lab = jnp.broadcast_to(labels_ref[t : t + 1, :], (128, 128)).T
            lab = jnp.concatenate([lab] * (width // 128), axis=1)
            logits = acc[t * 128 : (t + 1) * 128, :]
            top = jnp.max(logits, axis=1, keepdims=True)
            exps = jnp.exp(logits - top)
            denom = jnp.sum(exps, axis=1, keepdims=True)
            onehot = (lab == classes).astype(F32)
            picked = jnp.sum(logits * onehot, axis=1, keepdims=True)
            probs = exps / denom
            slopes[0, t * 128 : (t + 1) * 128, :] = ((probs - onehot) / tokens).astype(BF16)
            term = top + jnp.log(denom) - picked
            loss_lanes += jnp.sum(jnp.broadcast_to(term, (128, 128)), axis=0, keepdims=True)

    send(slopes.at[0], slopes.at[1], ss_sem.at[0], sr_sem.at[0], dp_of(0, 0, 1))
    pl.semaphore_wait(mid1, 2)
    pl.semaphore_signal(mid2, inc=1, device_id={"layer": away}, device_id_type=MESH)

    def outer(left, right):
        return lax.dot_general(
            left, right, (((0,), (0,)), ((), ())), preferred_element_type=F32
        )

    def near_tokens(k, carry):
        cols = pl.multiple_of(k * chip + c * 384, 128)
        part[k] = outer(a_v[:, pl.ds(cols, 512)], slopes[0])
        return carry

    with jax.named_scope("own_tokens"):
        lax.fori_loop(0, 8, near_tokens, 0)
    with jax.named_scope("partner"):
        for k in range(8):
            arrived(a_far.at[k], ar_sem.at[k])
        arrived(slopes.at[1], sr_sem.at[0])

    def at(dx, dy):
        return ((x + dx) % 2) * 4 + (y + dy) % 4

    def far_tokens(dx, dy):
        k = at(dx, dy)
        part[k] += outer(a_far[k], slopes[1])

    def partial(dx, dy, q):
        return part[at(dx, dy), pl.ds(pl.multiple_of(c * 64 + q * quarter, 16), quarter), :]

    def ship(i, value, dest):
        top = jnp.maximum(jnp.max(jnp.abs(value), axis=0, keepdims=True), 1e-30)
        sbuf[i] = jnp.round(value * (32767.0 / top)).astype(jnp.int32).astype(jnp.int16)
        sscale[i] = top * (1.0 / 32767.0)
        send(sbuf.at[i], rbuf.at[i], ms_sem.at[i, 0], mr_sem.at[i, 0], dp_of(*dest))
        send(sscale.at[i], rscale.at[i], ms_sem.at[i, 1], mr_sem.at[i, 1], dp_of(*dest))

    def got(i):
        arrived(rbuf.at[i], mr_sem.at[i, 0])
        arrived(rscale.at[i], mr_sem.at[i, 1])
        return rbuf[i].astype(jnp.int32).astype(F32) * rscale[i]

    def x_first(dy, q):
        return dy * 2 + q

    def x_last(q):
        return 8 + q - 2

    def base(side):
        return 10 if side == UP else 19

    def two(side, kind):
        return base(side) + kind

    def one(side, kind, q):
        return base(side) + 3 + kind * 2 + q % 2

    with jax.named_scope("rs_a"):
        far_tokens(1, 2)
        ship(two(UP, 1), partial(1, 2, 2), UP)
        ship(two(DOWN, 1), partial(1, 2, 3), DOWN)
        for q in (0, 1):
            ship(x_first(2, q), partial(1, 2, q), X)
        far_tokens(0, 2)
        ship(two(UP, 0), partial(0, 2, 2), UP)
        ship(two(DOWN, 0), partial(0, 2, 3), DOWN)
    with jax.named_scope("rs_b"):
        far_tokens(1, 1)
        ship(one(UP, 1, 3), partial(1, 1, 3), UP)
        far_tokens(1, 3)
        ship(one(DOWN, 1, 2), partial(1, 3, 2), DOWN)
        ship(x_first(1, 1), partial(1, 1, 1), X)
        ship(x_first(3, 0), partial(1, 3, 0), X)
        far_tokens(0, 1)
        ship(one(UP, 0, 3), partial(0, 1, 3), UP)
        far_tokens(0, 3)
        ship(one(DOWN, 0, 2), partial(0, 3, 2), DOWN)
        ship(x_first(1, 0), partial(1, 1, 0), X)
        ship(x_first(3, 1), partial(1, 3, 1), X)
        far_tokens(1, 0)
        for q in (0, 1):
            ship(x_first(0, q), partial(1, 0, q), X)
        far_tokens(0, 0)
    with jax.named_scope("rs_c"):
        for kind in (1, 0):
            ship(one(UP, kind, 2), partial(kind, 1, 2) + got(two(UP, kind)), UP)
            ship(one(DOWN, kind, 3), partial(kind, 3, 3) + got(two(DOWN, kind)), DOWN)
    with jax.named_scope("rs_d"):
        ship(two(UP, 2), partial(0, 2, 0) + got(x_first(2, 0)), UP)
        ship(two(DOWN, 2), partial(0, 2, 1) + got(x_first(2, 1)), DOWN)
    with jax.named_scope("rs_e"):
        ship(one(UP, 2, 1), partial(0, 1, 1) + got(x_first(1, 1)), UP)
        ship(one(DOWN, 2, 0), partial(0, 3, 0) + got(x_first(3, 0)), DOWN)
    with jax.named_scope("rs_f"):
        pl.semaphore_wait(mid2, 1)
        for q in (3, 2):
            ship(x_last(q), partial(1, 0, q) + got(one(UP, 1, q)) + got(one(DOWN, 1, q)), X)
    with jax.named_scope("rs_g"):
        ship(one(UP, 2, 0), partial(0, 1, 0) + got(x_first(1, 0)) + got(two(UP, 2)), UP)
        ship(one(DOWN, 2, 1), partial(0, 3, 1) + got(x_first(3, 1)) + got(two(DOWN, 2)), DOWN)

    def finish(q, total, carry):
        for g in range(quarter // 8):
            for j in range(4):
                v = total[g * 8 : (g + 1) * 8, j * 128 : (j + 1) * 128]
                grad_ref[pl.ds((q * quarter + g * 8) * 4 + j, 8, stride=4), :] = v
                carry = carry + v * v
        return carry

    square = jnp.zeros((8, 128), F32)
    with jax.named_scope("fin_a"):
        for q in (3, 2):
            total = partial(0, 0, q) + got(one(UP, 0, q)) + got(one(DOWN, 0, q))
            part[at(0, 0), pl.ds(pl.multiple_of(c * 64 + q * quarter, 16), quarter), :] = total
        for q in (0, 1):
            total = partial(0, 0, q) + got(x_first(0, q))
            part[at(0, 0), pl.ds(pl.multiple_of(c * 64 + q * quarter, 16), quarter), :] = total
    with jax.named_scope("fin_b"):
        for q in (1, 0):
            total = partial(0, 0, q) + got(one(UP, 2, q)) + got(one(DOWN, 2, q))
            square = finish(q, total, square)
    with jax.named_scope("fin_c"):
        for q in (3, 2):
            square = finish(q, partial(0, 0, q) + got(x_last(q)), square)
        tile = jnp.concatenate(
            [jnp.sum(square, axis=0, keepdims=True), loss_lanes, jnp.zeros((6, 128), F32)], axis=0
        )

    def spread(slots, here, index, peers, ssem, rsem):
        slots[index] = here
        copies = []
        for k, who in enumerate(peers):
            cp = pltpu.make_async_remote_copy(
                src_ref=slots.at[index], dst_ref=slots.at[index], send_sem=ssem.at[k],
                recv_sem=rsem.at[k], device_id=who, device_id_type=MESH,
            )
            cp.start()
            copies.append(cp)
        while sent:
            sent.pop().wait_send()
        for cp in copies:
            cp.wait()
        return jnp.sum(slots[...], axis=0)

    m = y * 2 + c
    n = x * 8 + lay
    with jax.named_scope("red1"):
        tile = spread(
            slots1, tile, m, [{"dp": x * 8 + (m + k) % 8} for k in range(1, 8)], p1s, p1r
        )
    with jax.named_scope("red2"):
        others = [(n + k) % 16 for k in range(1, 16)]
        sums = spread(
            slots2, tile, n, [{"dp": o // 8 * 8 + m, "layer": o % 8} for o in others], p2s, p2r
        )
    square = jnp.broadcast_to(jnp.sum(sums[0:1, :], axis=1, keepdims=True), (1, 128))
    factor_ref[...] = jnp.minimum(1.0, 0.25 / jnp.sqrt(square + 1e-12))
    loss_ref[...] = sums[1:2, :] / (tokens * 8)


def shards(activations, labels, weights, first_moment, second_moment):
    tok = activations.shape[0]
    depth = activations.shape[2]
    rows, _, width = weights.shape
    tokens = tok * lax.axis_size("dp")
    dma = pltpu.SemaphoreType.DMA
    vmem = pltpu.VMEM
    lines = rows * width // 128
    anywhere = pl.BlockSpec(memory_space=pltpu.MemorySpace.HBM)
    inside = pl.BlockSpec(memory_space=pltpu.VMEM)

    def body(*refs):
        kernel(tokens, *refs)

    grad, factor, loss = pl.pallas_call(
        body,
        out_shape=(
            jax.ShapeDtypeStruct((lines, 128), F32),
            jax.ShapeDtypeStruct((1, 128), F32),
            jax.ShapeDtypeStruct((1, 128), F32),
        ),
        in_specs=[anywhere, anywhere, anywhere],
        out_specs=(inside, inside, inside),
        scratch_shapes=[
            vmem((tok, depth), BF16),
            vmem((tok // 128, 128), jnp.int32),
            vmem((lines, 128), F32),
            vmem((depth, width), BF16),
            vmem((8, tok, 512), BF16),
            vmem((2, tok, width), BF16),
            vmem((tok, width), F32),
            vmem((8, 512, width), F32),
            vmem((28, rows // 4, width), jnp.int16),
            vmem((28, rows // 4, width), jnp.int16),
            vmem((28, 1, width), F32),
            vmem((28, 1, width), F32),
            vmem((8, 8, 128), F32),
            vmem((16, 8, 128), F32),
            dma((3,)),
            dma((28,)),
            dma((8, 4)),
            dma((8, 4)),
            dma((8, 4)),
            dma((8,)),
            dma((8,)),
            dma((1,)),
            dma((1,)),
            dma((28, 2)),
            dma((28, 2)),
            dma((7,)),
            dma((7,)),
            dma((15,)),
            dma((15,)),
            pltpu.SemaphoreType.REGULAR,
            pltpu.SemaphoreType.REGULAR,
        ],
        compiler_params=pltpu.CompilerParams(
            collective_id=0, has_side_effects=True, vmem_limit_bytes=48 << 20
        ),
        name="probe_step",
    )(
        *(
            pltpu.with_memory_space_constraint(v, pltpu.MemorySpace.HBM)
            for v in (
                activations.reshape(tok, depth),
                labels.reshape(tok // 128, 128),
                weights.reshape(lines, 128),
            )
        )
    )
    held = [v.reshape(lines, 128) for v in (weights, first_moment, second_moment)]
    grad, weights, first_moment, second_moment = lax.optimization_barrier((grad, *held))
    clipped = factor * grad
    new_first = 0.9 * first_moment + 0.1 * clipped
    new_second = 0.999 * second_moment + 0.001 * clipped * clipped
    new_weights = weights - 0.001 * (new_first / (1.0 - 0.9**STEP)) / (
        jnp.sqrt(new_second / (1.0 - 0.999**STEP)) + 1e-08
    )
    outs = (v.reshape(rows, 1, width) for v in (new_weights, new_first, new_second))
    return (*outs, loss[0, 0])


def solution(mesh):
    rows = P("dp", "layer", None)
    return jax.shard_map(
        shards,
        mesh=mesh,
        in_specs=(rows, P("dp"), rows, rows, rows),
        out_specs=(rows, rows, rows, P()),
        check_vma=False,
    )
```

time: 94.7 us -> 80.8 us (0.85)
  Pallas kernels: 90.8 us -> 76.9 us
    pallas_call x1, Pallas kernels: 90.8 us -> 76.9 us  [shards(): pl.pallas_call(body, out_shape=(jax.ShapeDtypeStruct((lines, 128), F32),...]
where the time goes in v4:
time: 80.8 us; the launch traced here: 80.7 us
  Pallas kernels  76.9 us (95%)
  other arithmetic  1.96 us (2%)
  between operations  1.85 us (2%)
    pallas_call x1, Pallas kernels, shards(): pl.pallas_call(body, out_shape=(jax.ShapeDtypeStruct((lines, 128), F32),...  76.9 us
    sub x1, other arithmetic, shards(): weights - 0.001 * (new_first / (1.0 - 0.9 ** STEP)) / (jnp.sqrt(new_secon...  1.96 us

profile of v4, /device:TPU:1, one launch (start us, length us, event | category | flops | bytes accessed | tf_op | source)
XLA Modules:
  0.0 80.7 jit_solution(5960921413966295689)
XLA Ops:
  0.6 0.0 copy-start.2
  0.6 0.0 copy-start.1
  0.7 0.0 copy-start
  0.7 76.9 %probe_step.1 = (f32[1792,128]{1,0:T(8,128)S(1)}, f32[1,128]{1,0:T(1,128)S(1)}, f32[1,128]{1,0:T(1,128)S(1)}) custom-call(bf16[256,7168]{1,0:T(8,128)(2,1)} %bitcast.15, s32[2,128]{1,0:T(2,128)} %bitcast.21, f32[1792,128]{1,0:T(8,128)} %bitcast.13), custom_call_target="tpu_custom_call" | custom-call | tf_op jit(solution)/shard_map/probe_step/pallas_call | solution.py:415
  77.6 0.0 copy-done.2
  77.6 0.0 copy-done.1
  77.6 0.0 copy-done
  77.6 2.0 %divide_subtract_fusion = (f32[1792,128]{1,0:T(8,128)}, f32[1792,128]{1,0:T(8,128)}, f32[1792,128]{1,0:T(8,128)}) fusion(f32[1792,128]{1,0:T(8,128)S(1)} %bitcast.14, f32[1792,128]{1,0:T(8,128)S(1)} %get-tuple-element.15, f32[128]{0:T(128)S(1)} %bitcast.11, f32[1792,128]{1,0:T(8,128)S(1)} %bitcast.16, f32[1792,128]{1,0:T(8,128)S(1)} %bitcast.17), kind=kLoop, calls=%fused_computation.2 | loop fusion | flops 2981888 | bytes 6423040 | tf_op jit(solution)/shard_map/sub | solution.py:476
Async XLA Ops:
  0.6 76.9 %copy-start.2 = (f32[448,1,512]{2,1,0:T(1,128)S(1)}, f32[448,1,512]{2,1,0:T(1,128)}, u32[]{:S(2)}) copy-start(f32[448,1,512]{2,1,0:T(1,128)} %param.9) | copy-start | bytes 2752516
  0.6 76.9 %copy-start.1 = (f32[448,1,512]{2,1,0:T(1,128)S(1)}, f32[448,1,512]{2,1,0:T(1,128)}, u32[]{:S(2)}) copy-start(f32[448,1,512]{2,1,0:T(1,128)} %param.8) | copy-start | bytes 2752516
  0.7 76.9 %copy-start = (f32[448,1,512]{2,1,0:T(1,128)S(1)}, f32[448,1,512]{2,1,0:T(1,128)}, u32[]{:S(2)}) copy-start(f32[448,1,512]{2,1,0:T(1,128)} %param.7) | copy-start | bytes 2752516

commit v5 on v4

--- a/solution.py
+++ b/solution.py
@@ -22,6 +22,7 @@
     a_v,
     labels_ref,
     w32,
+    grad_v,
     wbuf,
     a_far,
     slopes,
@@ -34,27 +35,21 @@
     slots1,
     slots2,
     ld_sem,
-    ws_sem,
+    sent_sem,
     wr_sem,
-    ds_sem,
     dr_sem,
-    as_sem,
     ar_sem,
-    ss_sem,
     sr_sem,
-    ms_sem,
     mr_sem,
-    p1s,
-    p1r,
-    p2s,
-    p2r,
+    red_sem,
     mid1,
     mid2,
 ):
     tok = a_v.shape[0]
     width = wbuf.shape[1]
     rows = wbuf.shape[0] // 16
-    quarter = rows // 4
+    starts, sizes = (0, 96, 192, 320), (96, 96, 128, 128)
+    w_starts, w_sizes = (0, 128, 256, 352), (128, 128, 96, 96)
     chip = 2 * rows
     d = lax.axis_index("dp")
     lay = lax.axis_index("layer")
@@ -101,7 +96,6 @@
         with jax.named_scope("barrier"):
             pl.semaphore_wait(barrier, len(near))
 
-    sent = []
 
     def copy_of(src, dst, ssem, rsem, dp):
         return pltpu.make_async_remote_copy(
@@ -109,31 +103,29 @@
             device_id={"dp": dp}, device_id_type=MESH,
         )
 
-    def send(*what):
-        cp = copy_of(*what)
-        cp.start()
-        sent.append(cp)
+    def send(family, src, dst, rsem, dp):
+        copy_of(src, dst, sent_sem.at[family], rsem, dp).start()
+
+    def all_sent(family, like):
+        copy_of(like, like, sent_sem.at[family], sent_sem.at[family], dp_of(0, 0, 1)).wait_send()
 
     def arrived(ref, rsem):
-        copy_of(ref, ref, ws_sem.at[0], rsem, dp_of(0, 0, 1)).wait_recv()
+        copy_of(ref, ref, sent_sem.at[0], rsem, dp_of(0, 0, 1)).wait_recv()
 
     def w_rows(dx, dy, dc, q):
-        start = pl.multiple_of(dp_of(dx, dy, dc) * rows + q * quarter, 16)
-        return wbuf.at[pl.ds(start, quarter), :]
-
-    wcount = [0]
+        start = pl.multiple_of(dp_of(dx, dy, dc) * rows + w_starts[q], 32)
+        return wbuf.at[pl.ds(start, w_sizes[q]), :]
 
     def w_send(dx, dy, q, *targets):
         ref = w_rows(dx, dy, 0, q)
         for tx, ty in targets:
             k = ((dx - tx) % 2) * 4 + (dy - ty) % 4
-            send(ref, ref, ws_sem.at[wcount[0]], wr_sem.at[k, q], dp_of(tx, ty))
-            wcount[0] += 1
+            send(0, ref, ref, wr_sem.at[k, q], dp_of(tx, ty))
 
     def w_pass(dx, dy, q):
         ref = w_rows(dx, dy, 0, q)
         k = dx * 4 + dy
-        send(ref, ref, ds_sem.at[k, q], dr_sem.at[k, q], dp_of(0, 0, 1))
+        send(1, ref, ref, dr_sem.at[k], dp_of(0, 0, 1))
 
     def w_take(dx, dy, q, *targets):
         arrived(w_rows(dx, dy, 0, q), wr_sem.at[dx * 4 + dy, q])
@@ -147,8 +139,8 @@
 
     def logits_of(dx, dy):
         cols = chip_cols(dx, dy)
-        for q in range(4):
-            arrived(w_rows(dx, dy, 1, q), dr_sem.at[dx * 4 + dy, q])
+        start = pl.multiple_of(dp_of(dx, dy, 1) * rows, 32)
+        arrived(wbuf.at[pl.ds(start, rows), :], dr_sem.at[dx * 4 + dy])
 
         def step(n, carry):
             lanes = pl.ds(pl.multiple_of(n * 256, 256), 256)
@@ -173,10 +165,7 @@
             w_pass(0, 0, q)
         for k in range(8):
             start = pl.multiple_of(k * chip + (1 - c) * 384, 128)
-            send(
-                a_hbm.at[:, pl.ds(start, 512)], a_far.at[k], as_sem.at[k], ar_sem.at[k],
-                dp_of(0, 0, 1),
-            )
+            send(2, a_hbm.at[:, pl.ds(start, 512)], a_far.at[k], ar_sem.at[0], dp_of(0, 0, 1))
         load_a.wait()
         load_labels.wait()
 
@@ -237,7 +226,7 @@
             term = top + jnp.log(denom) - picked
             loss_lanes += jnp.sum(jnp.broadcast_to(term, (128, 128)), axis=0, keepdims=True)
 
-    send(slopes.at[0], slopes.at[1], ss_sem.at[0], sr_sem.at[0], dp_of(0, 0, 1))
+    send(3, slopes.at[0], slopes.at[1], sr_sem.at[0], dp_of(0, 0, 1))
     pl.semaphore_wait(mid1, 2)
     pl.semaphore_signal(mid2, inc=1, device_id={"layer": away}, device_id_type=MESH)
 
@@ -251,34 +240,43 @@
         part[k] = outer(a_v[:, pl.ds(cols, 512)], slopes[0])
         return carry
 
-    with jax.named_scope("own_tokens"):
-        lax.fori_loop(0, 8, near_tokens, 0)
-    with jax.named_scope("partner"):
-        for k in range(8):
-            arrived(a_far.at[k], ar_sem.at[k])
-        arrived(slopes.at[1], sr_sem.at[0])
-
     def at(dx, dy):
         return ((x + dx) % 2) * 4 + (y + dy) % 4
 
-    def far_tokens(dx, dy):
+    ahead = ((1, 2), (0, 2), (1, 1), (1, 3))
+
+    def tokens_of(dx, dy):
         k = at(dx, dy)
+        if (dx, dy) not in ahead:
+            near_tokens(k, 0)
         part[k] += outer(a_far[k], slopes[1])
 
+    with jax.named_scope("own_tokens"):
+        for who in ahead:
+            near_tokens(at(*who), 0)
+    with jax.named_scope("partner"):
+        arrived(a_far, ar_sem.at[0])
+        arrived(slopes.at[1], sr_sem.at[0])
+
+    def block_rows(q):
+        return pl.ds(pl.multiple_of(c * 64 + starts[q], 32), sizes[q])
+
     def partial(dx, dy, q):
-        return part[at(dx, dy), pl.ds(pl.multiple_of(c * 64 + q * quarter, 16), quarter), :]
+        return part[at(dx, dy), block_rows(q), :]
 
     def ship(i, value, dest):
         top = jnp.maximum(jnp.max(jnp.abs(value), axis=0, keepdims=True), 1e-30)
-        sbuf[i] = jnp.round(value * (32767.0 / top)).astype(jnp.int32).astype(jnp.int16)
+        held = pl.ds(0, value.shape[0])
+        sbuf[i, held, :] = jnp.round(value * (32767.0 / top)).astype(jnp.int32).astype(jnp.int16)
         sscale[i] = top * (1.0 / 32767.0)
-        send(sbuf.at[i], rbuf.at[i], ms_sem.at[i, 0], mr_sem.at[i, 0], dp_of(*dest))
-        send(sscale.at[i], rscale.at[i], ms_sem.at[i, 1], mr_sem.at[i, 1], dp_of(*dest))
-
-    def got(i):
-        arrived(rbuf.at[i], mr_sem.at[i, 0])
+        send(4, sbuf.at[i, held, :], rbuf.at[i, held, :], mr_sem.at[i, 0], dp_of(*dest))
+        send(5, sscale.at[i], rscale.at[i], mr_sem.at[i, 1], dp_of(*dest))
+
+    def got(i, q):
+        held = pl.ds(0, sizes[q])
+        arrived(rbuf.at[i, held, :], mr_sem.at[i, 0])
         arrived(rscale.at[i], mr_sem.at[i, 1])
-        return rbuf[i].astype(jnp.int32).astype(F32) * rscale[i]
+        return rbuf[i, held, :].astype(jnp.int32).astype(F32) * rscale[i]
 
     def x_first(dy, q):
         return dy * 2 + q
@@ -296,103 +294,110 @@
         return base(side) + 3 + kind * 2 + q % 2
 
     with jax.named_scope("rs_a"):
-        far_tokens(1, 2)
+        tokens_of(1, 2)
         ship(two(UP, 1), partial(1, 2, 2), UP)
         ship(two(DOWN, 1), partial(1, 2, 3), DOWN)
         for q in (0, 1):
             ship(x_first(2, q), partial(1, 2, q), X)
-        far_tokens(0, 2)
+        tokens_of(0, 2)
         ship(two(UP, 0), partial(0, 2, 2), UP)
         ship(two(DOWN, 0), partial(0, 2, 3), DOWN)
     with jax.named_scope("rs_b"):
-        far_tokens(1, 1)
+        tokens_of(1, 1)
+        ship(x_first(1, 1), partial(1, 1, 1), X)
         ship(one(UP, 1, 3), partial(1, 1, 3), UP)
-        far_tokens(1, 3)
+        tokens_of(1, 3)
+        ship(x_first(3, 0), partial(1, 3, 0), X)
         ship(one(DOWN, 1, 2), partial(1, 3, 2), DOWN)
-        ship(x_first(1, 1), partial(1, 1, 1), X)
-        ship(x_first(3, 0), partial(1, 3, 0), X)
-        far_tokens(0, 1)
+        tokens_of(0, 1)
         ship(one(UP, 0, 3), partial(0, 1, 3), UP)
-        far_tokens(0, 3)
+        tokens_of(0, 3)
         ship(one(DOWN, 0, 2), partial(0, 3, 2), DOWN)
         ship(x_first(1, 0), partial(1, 1, 0), X)
         ship(x_first(3, 1), partial(1, 3, 1), X)
-        far_tokens(1, 0)
+        tokens_of(1, 0)
         for q in (0, 1):
             ship(x_first(0, q), partial(1, 0, q), X)
-        far_tokens(0, 0)
+        tokens_of(0, 0)
     with jax.named_scope("rs_c"):
         for kind in (1, 0):
-            ship(one(UP, kind, 2), partial(kind, 1, 2) + got(two(UP, kind)), UP)
-            ship(one(DOWN, kind, 3), partial(kind, 3, 3) + got(two(DOWN, kind)), DOWN)
+            ship(one(UP, kind, 2), partial(kind, 1, 2) + got(two(UP, kind), 2), UP)
+            ship(one(DOWN, kind, 3), partial(kind, 3, 3) + got(two(DOWN, kind), 3), DOWN)
     with jax.named_scope("rs_d"):
-        ship(two(UP, 2), partial(0, 2, 0) + got(x_first(2, 0)), UP)
-        ship(two(DOWN, 2), partial(0, 2, 1) + got(x_first(2, 1)), DOWN)
+        ship(two(UP, 2), partial(0, 2, 0) + got(x_first(2, 0), 0), UP)
+        ship(two(DOWN, 2), partial(0, 2, 1) + got(x_first(2, 1), 1), DOWN)
     with jax.named_scope("rs_e"):
-        ship(one(UP, 2, 1), partial(0, 1, 1) + got(x_first(1, 1)), UP)
-        ship(one(DOWN, 2, 0), partial(0, 3, 0) + got(x_first(3, 0)), DOWN)
+        ship(one(UP, 2, 1), partial(0, 1, 1) + got(x_first(1, 1), 1), UP)
+        ship(one(DOWN, 2, 0), partial(0, 3, 0) + got(x_first(3, 0), 0), DOWN)
     with jax.named_scope("rs_f"):
         pl.semaphore_wait(mid2, 1)
         for q in (3, 2):
-            ship(x_last(q), partial(1, 0, q) + got(one(UP, 1, q)) + got(one(DOWN, 1, q)), X)
+            ship(x_last(q), partial(1, 0, q) + got(one(UP, 1, q), q) + got(one(DOWN, 1, q), q), X)
     with jax.named_scope("rs_g"):
-        ship(one(UP, 2, 0), partial(0, 1, 0) + got(x_first(1, 0)) + got(two(UP, 2)), UP)
-        ship(one(DOWN, 2, 1), partial(0, 3, 1) + got(x_first(3, 1)) + got(two(DOWN, 2)), DOWN)
+        ship(one(UP, 2, 0), partial(0, 1, 0) + got(x_first(1, 0), 0) + got(two(UP, 2), 0), UP)
+        ship(one(DOWN, 2, 1), partial(0, 3, 1) + got(x_first(3, 1), 1) + got(two(DOWN, 2), 1), DOWN)
 
     def finish(q, total, carry):
-        for g in range(quarter // 8):
+        for g in range(sizes[q] // 8):
             for j in range(4):
                 v = total[g * 8 : (g + 1) * 8, j * 128 : (j + 1) * 128]
-                grad_ref[pl.ds((q * quarter + g * 8) * 4 + j, 8, stride=4), :] = v
+                grad_v[pl.ds((starts[q] + g * 8) * 4 + j, 8, stride=4), :] = v
                 carry = carry + v * v
         return carry
 
     square = jnp.zeros((8, 128), F32)
     with jax.named_scope("fin_a"):
         for q in (3, 2):
-            total = partial(0, 0, q) + got(one(UP, 0, q)) + got(one(DOWN, 0, q))
-            part[at(0, 0), pl.ds(pl.multiple_of(c * 64 + q * quarter, 16), quarter), :] = total
+            total = partial(0, 0, q) + got(one(UP, 0, q), q) + got(one(DOWN, 0, q), q)
+            part[at(0, 0), block_rows(q), :] = total
         for q in (0, 1):
-            total = partial(0, 0, q) + got(x_first(0, q))
-            part[at(0, 0), pl.ds(pl.multiple_of(c * 64 + q * quarter, 16), quarter), :] = total
+            part[at(0, 0), block_rows(q), :] = partial(0, 0, q) + got(x_first(0, q), q)
     with jax.named_scope("fin_b"):
         for q in (1, 0):
-            total = partial(0, 0, q) + got(one(UP, 2, q)) + got(one(DOWN, 2, q))
+            total = partial(0, 0, q) + got(one(UP, 2, q), q) + got(one(DOWN, 2, q), q)
             square = finish(q, total, square)
     with jax.named_scope("fin_c"):
         for q in (3, 2):
-            square = finish(q, partial(0, 0, q) + got(x_last(q)), square)
+            square = finish(q, partial(0, 0, q) + got(x_last(q), q), square)
         tile = jnp.concatenate(
             [jnp.sum(square, axis=0, keepdims=True), loss_lanes, jnp.zeros((6, 128), F32)], axis=0
         )
-
-    def spread(slots, here, index, peers, ssem, rsem):
+        store = pltpu.make_async_copy(grad_v, grad_ref, ld_sem.at[3])
+        store.start()
+
+    def spread(slots, here, index, peers, stage):
         slots[index] = here
-        copies = []
-        for k, who in enumerate(peers):
-            cp = pltpu.make_async_remote_copy(
-                src_ref=slots.at[index], dst_ref=slots.at[index], send_sem=ssem.at[k],
-                recv_sem=rsem.at[k], device_id=who, device_id_type=MESH,
-            )
-            cp.start()
-            copies.append(cp)
-        while sent:
-            sent.pop().wait_send()
-        for cp in copies:
-            cp.wait()
+        for who in peers:
+            pltpu.make_async_remote_copy(
+                src_ref=slots.at[index], dst_ref=slots.at[index], send_sem=sent_sem.at[6 + stage],
+                recv_sem=red_sem.at[stage], device_id=who, device_id_type=MESH,
+            ).start()
+        if stage == 0:
+            moved = 7 * rows
+            all_sent(0, wbuf.at[pl.ds(0, moved), :])
+            all_sent(1, wbuf.at[pl.ds(0, 8 * rows), :])
+            all_sent(2, a_far)
+            all_sent(3, slopes.at[0])
+            all_sent(4, wbuf.at[pl.ds(0, moved), :])
+            all_sent(5, sscale)
+        some = slots.at[pl.ds(0, len(peers))]
+        arrived(some, red_sem.at[stage])
+        all_sent(6 + stage, some)
         return jnp.sum(slots[...], axis=0)
 
     m = y * 2 + c
     n = x * 8 + lay
     with jax.named_scope("red1"):
         tile = spread(
-            slots1, tile, m, [{"dp": x * 8 + (m + k) % 8} for k in range(1, 8)], p1s, p1r
+            slots1, tile, m, [{"dp": x * 8 + (m + k) % 8} for k in range(1, 8)], 0
         )
     with jax.named_scope("red2"):
         others = [(n + k) % 16 for k in range(1, 16)]
         sums = spread(
-            slots2, tile, n, [{"dp": o // 8 * 8 + m, "layer": o % 8} for o in others], p2s, p2r
-        )
+            slots2, tile, n, [{"dp": o // 8 * 8 + m, "layer": o % 8} for o in others], 1
+        )
+    with jax.named_scope("end1"):
+        store.wait()
     square = jnp.broadcast_to(jnp.sum(sums[0:1, :], axis=1, keepdims=True), (1, 128))
     factor_ref[...] = jnp.minimum(1.0, 0.25 / jnp.sqrt(square + 1e-12))
     loss_ref[...] = sums[1:2, :] / (tokens * 8)
@@ -420,37 +425,31 @@
             jax.ShapeDtypeStruct((1, 128), F32),
         ),
         in_specs=[anywhere, anywhere, anywhere],
-        out_specs=(inside, inside, inside),
+        out_specs=(anywhere, inside, inside),
         scratch_shapes=[
             vmem((tok, depth), BF16),
             vmem((tok // 128, 128), jnp.int32),
+            vmem((lines, 128), F32),
             vmem((lines, 128), F32),
             vmem((depth, width), BF16),
             vmem((8, tok, 512), BF16),
             vmem((2, tok, width), BF16),
             vmem((tok, width), F32),
             vmem((8, 512, width), F32),
-            vmem((28, rows // 4, width), jnp.int16),
-            vmem((28, rows // 4, width), jnp.int16),
+            vmem((28, 128, width), jnp.int16),
+            vmem((28, 128, width), jnp.int16),
             vmem((28, 1, width), F32),
             vmem((28, 1, width), F32),
             vmem((8, 8, 128), F32),
             vmem((16, 8, 128), F32),
-            dma((3,)),
-            dma((28,)),
+            dma((4,)),
+            dma((8,)),
             dma((8, 4)),
-            dma((8, 4)),
-            dma((8, 4)),
-            dma((8,)),
             dma((8,)),
             dma((1,)),
             dma((1,)),
             dma((28, 2)),
-            dma((28, 2)),
-            dma((7,)),
-            dma((7,)),
-            dma((15,)),
-            dma((15,)),
+            dma((2,)),
             pltpu.SemaphoreType.REGULAR,
             pltpu.SemaphoreType.REGULAR,
         ],

time: 80.8 us -> 78.2 us (0.968)
  Pallas kernels: 76.9 us -> 74.2 us
    pallas_call x1, Pallas kernels: 76.9 us -> 74.2 us  [shards(): pl.pallas_call(body, out_shape=(jax.ShapeDtypeStruct((lines, 128), F32),...]
where the time goes in v5:
time: 78.2 us; the launch traced here: 78.1 us
  Pallas kernels  74.2 us (95%)
  other arithmetic  1.96 us (3%)
  between operations  1.85 us (2%)
    pallas_call x1, Pallas kernels, shards(): pl.pallas_call(body, out_shape=(jax.ShapeDtypeStruct((lines, 128), F32),...  74.2 us
    sub x1, other arithmetic, shards(): weights - 0.001 * (new_first / (1.0 - 0.9 ** STEP)) / (jnp.sqrt(new_secon...  1.96 us

profile of v5, /device:TPU:1, one launch (start us, length us, event | category | flops | bytes accessed | tf_op | source)
XLA Modules:
  0.0 78.1 jit_solution(3282581050993692371)
XLA Ops:
  0.6 0.0 copy-start.2
  0.6 0.0 copy-start.1
  0.7 0.0 copy-start
  0.7 74.2 %probe_step.1 = (f32[1792,128]{1,0:T(8,128)S(1)}, f32[1,128]{1,0:T(1,128)S(1)}, f32[1,128]{1,0:T(1,128)S(1)}) custom-call(bf16[256,7168]{1,0:T(8,128)(2,1)} %bitcast.15, s32[2,128]{1,0:T(2,128)} %bitcast.21, f32[1792,128]{1,0:T(8,128)} %bitcast.13), custom_call_target="tpu_custom_call" | custom-call | tf_op jit(solution)/shard_map/probe_step/pallas_call | solution.py:420
  74.9 0.0 copy-done.2
  74.9 0.0 copy-done.1
  74.9 0.0 copy-done
  74.9 2.0 %divide_subtract_fusion = (f32[1792,128]{1,0:T(8,128)}, f32[1792,128]{1,0:T(8,128)}, f32[1792,128]{1,0:T(8,128)}) fusion(f32[1792,128]{1,0:T(8,128)S(1)} %bitcast.14, f32[1792,128]{1,0:T(8,128)S(1)} %get-tuple-element.15, f32[128]{0:T(128)S(1)} %bitcast.11, f32[1792,128]{1,0:T(8,128)S(1)} %bitcast.16, f32[1792,128]{1,0:T(8,128)S(1)} %bitcast.17), kind=kLoop, calls=%fused_computation.2 | loop fusion | flops 2981888 | bytes 6423040 | tf_op jit(solution)/shard_map/sub | solution.py:475
Async XLA Ops:
  0.6 74.3 %copy-start.2 = (f32[448,1,512]{2,1,0:T(1,128)S(1)}, f32[448,1,512]{2,1,0:T(1,128)}, u32[]{:S(2)}) copy-start(f32[448,1,512]{2,1,0:T(1,128)} %param.9) | copy-start | bytes 2752516
  0.6 74.3 %copy-start.1 = (f32[448,1,512]{2,1,0:T(1,128)S(1)}, f32[448,1,512]{2,1,0:T(1,128)}, u32[]{:S(2)}) copy-start(f32[448,1,512]{2,1,0:T(1,128)} %param.8) | copy-start | bytes 2752516
  0.7 74.3 %copy-start = (f32[448,1,512]{2,1,0:T(1,128)S(1)}, f32[448,1,512]{2,1,0:T(1,128)}, u32[]{:S(2)}) copy-start(f32[448,1,512]{2,1,0:T(1,128)} %param.7) | copy-start | bytes 2752516

commit v6 on v5

--- a/solution.py
+++ b/solution.py
@@ -223,10 +223,11 @@
             picked = jnp.sum(logits * onehot, axis=1, keepdims=True)
             probs = exps / denom
             slopes[0, t * 128 : (t + 1) * 128, :] = ((probs - onehot) / tokens).astype(BF16)
+            half = slopes.at[0, pl.ds(t * 128, 128), :]
+            send(3, half, slopes.at[1, pl.ds(t * 128, 128), :], sr_sem.at[0], dp_of(0, 0, 1))
             term = top + jnp.log(denom) - picked
             loss_lanes += jnp.sum(jnp.broadcast_to(term, (128, 128)), axis=0, keepdims=True)
 
-    send(3, slopes.at[0], slopes.at[1], sr_sem.at[0], dp_of(0, 0, 1))
     pl.semaphore_wait(mid1, 2)
     pl.semaphore_signal(mid2, inc=1, device_id={"layer": away}, device_id_type=MESH)
 
@@ -269,13 +270,12 @@
         held = pl.ds(0, value.shape[0])
         sbuf[i, held, :] = jnp.round(value * (32767.0 / top)).astype(jnp.int32).astype(jnp.int16)
         sscale[i] = top * (1.0 / 32767.0)
-        send(4, sbuf.at[i, held, :], rbuf.at[i, held, :], mr_sem.at[i, 0], dp_of(*dest))
-        send(5, sscale.at[i], rscale.at[i], mr_sem.at[i, 1], dp_of(*dest))
+        send(4, sbuf.at[i, held, :], rbuf.at[i, held, :], mr_sem.at[i], dp_of(*dest))
+        send(5, sscale.at[i], rscale.at[i], mr_sem.at[i], dp_of(*dest))
 
     def got(i, q):
         held = pl.ds(0, sizes[q])
-        arrived(rbuf.at[i, held, :], mr_sem.at[i, 0])
-        arrived(rscale.at[i], mr_sem.at[i, 1])
+        arrived(rscale.at[pl.ds(0, sizes[q] // 2 + 1)], mr_sem.at[i])
         return rbuf[i, held, :].astype(jnp.int32).astype(F32) * rscale[i]
 
     def x_first(dy, q):
@@ -319,13 +319,17 @@
         for q in (0, 1):
             ship(x_first(0, q), partial(1, 0, q), X)
         tokens_of(0, 0)
-    with jax.named_scope("rs_c"):
-        for kind in (1, 0):
-            ship(one(UP, kind, 2), partial(kind, 1, 2) + got(two(UP, kind), 2), UP)
-            ship(one(DOWN, kind, 3), partial(kind, 3, 3) + got(two(DOWN, kind), 3), DOWN)
+    def up_and_down(kind):
+        ship(one(UP, kind, 2), partial(kind, 1, 2) + got(two(UP, kind), 2), UP)
+        ship(one(DOWN, kind, 3), partial(kind, 3, 3) + got(two(DOWN, kind), 3), DOWN)
+
+    with jax.named_scope("rs_c1"):
+        up_and_down(1)
     with jax.named_scope("rs_d"):
         ship(two(UP, 2), partial(0, 2, 0) + got(x_first(2, 0), 0), UP)
         ship(two(DOWN, 2), partial(0, 2, 1) + got(x_first(2, 1), 1), DOWN)
+    with jax.named_scope("rs_c0"):
+        up_and_down(0)
     with jax.named_scope("rs_e"):
         ship(one(UP, 2, 1), partial(0, 1, 1) + got(x_first(1, 1), 1), UP)
         ship(one(DOWN, 2, 0), partial(0, 3, 0) + got(x_first(3, 0), 0), DOWN)
@@ -350,18 +354,16 @@
         for q in (3, 2):
             total = partial(0, 0, q) + got(one(UP, 0, q), q) + got(one(DOWN, 0, q), q)
             part[at(0, 0), block_rows(q), :] = total
-        for q in (0, 1):
-            part[at(0, 0), block_rows(q), :] = partial(0, 0, q) + got(x_first(0, q), q)
+        for q, side in ((1, UP), (0, DOWN)):
+            total = partial(0, 0, q) + got(x_first(0, q), q) + got(one(side, 2, q), q)
+            part[at(0, 0), block_rows(q), :] = total
     with jax.named_scope("fin_b"):
-        for q in (1, 0):
-            total = partial(0, 0, q) + got(one(UP, 2, q), q) + got(one(DOWN, 2, q), q)
-            square = finish(q, total, square)
-    with jax.named_scope("fin_c"):
         for q in (3, 2):
             square = finish(q, partial(0, 0, q) + got(x_last(q), q), square)
-        tile = jnp.concatenate(
-            [jnp.sum(square, axis=0, keepdims=True), loss_lanes, jnp.zeros((6, 128), F32)], axis=0
-        )
+    with jax.named_scope("fin_c"):
+        for q, side in ((0, UP), (1, DOWN)):
+            square = finish(q, partial(0, 0, q) + got(one(side, 2, q), q), square)
+        tile = jnp.concatenate([jnp.sum(square, axis=0, keepdims=True), loss_lanes], axis=1)
         store = pltpu.make_async_copy(grad_v, grad_ref, ld_sem.at[3])
         store.start()
 
@@ -398,9 +400,9 @@
         )
     with jax.named_scope("end1"):
         store.wait()
-    square = jnp.broadcast_to(jnp.sum(sums[0:1, :], axis=1, keepdims=True), (1, 128))
+    square = jnp.broadcast_to(jnp.sum(sums[:, 0:128], axis=1, keepdims=True), (1, 128))
     factor_ref[...] = jnp.minimum(1.0, 0.25 / jnp.sqrt(square + 1e-12))
-    loss_ref[...] = sums[1:2, :] / (tokens * 8)
+    loss_ref[...] = sums[:, 128:256] / (tokens * 8)
 
 
 def shards(activations, labels, weights, first_moment, second_moment):
@@ -439,16 +441,16 @@
             vmem((28, 128, width), jnp.int16),
             vmem((28, 128, width), jnp.int16),
             vmem((28, 1, width), F32),
-            vmem((28, 1, width), F32),
-            vmem((8, 8, 128), F32),
-            vmem((16, 8, 128), F32),
+            vmem((65, 1, width), F32),
+            vmem((8, 1, 256), F32),
+            vmem((16, 1, 256), F32),
             dma((4,)),
             dma((8,)),
             dma((8, 4)),
             dma((8,)),
             dma((1,)),
             dma((1,)),
-            dma((28, 2)),
+            dma((28,)),
             dma((2,)),
             pltpu.SemaphoreType.REGULAR,
             pltpu.SemaphoreType.REGULAR,

time: 78.2 us -> 77.1 us (0.986)
  Pallas kernels: 74.2 us -> 73.1 us
    pallas_call x1, Pallas kernels: 74.2 us -> 73.1 us  [shards(): pl.pallas_call(body, out_shape=(jax.ShapeDtypeStruct((lines, 128), F32),...]
where the time goes in v6:
time: 77.1 us; the launch traced here: 76.9 us
  Pallas kernels  73.1 us (95%)
  other arithmetic  1.96 us (3%)
  between operations  1.85 us (2%)
    pallas_call x1, Pallas kernels, shards(): pl.pallas_call(body, out_shape=(jax.ShapeDtypeStruct((lines, 128), F32),...  73.1 us
    sub x1, other arithmetic, shards(): weights - 0.001 * (new_first / (1.0 - 0.9 ** STEP)) / (jnp.sqrt(new_secon...  1.96 us

profile of v6, /device:TPU:1, one launch (start us, length us, event | category | flops | bytes accessed | tf_op | source)
XLA Modules:
  0.0 76.9 jit_solution(2104862255905630192)
XLA Ops:
  0.6 0.0 copy-start.2
  0.6 0.0 copy-start.1
  0.7 0.0 copy-start
  0.7 73.1 %probe_step.1 = (f32[1792,128]{1,0:T(8,128)S(1)}, f32[1,128]{1,0:T(1,128)S(1)}, f32[1,128]{1,0:T(1,128)S(1)}) custom-call(bf16[256,7168]{1,0:T(8,128)(2,1)} %bitcast.15, s32[2,128]{1,0:T(2,128)} %bitcast.21, f32[1792,128]{1,0:T(8,128)} %bitcast.13), custom_call_target="tpu_custom_call" | custom-call | tf_op jit(solution)/shard_map/probe_step/pallas_call | solution.py:422
  73.8 0.0 copy-done.2
  73.8 0.0 copy-done.1
  73.8 0.0 copy-done
  73.8 2.0 %divide_subtract_fusion = (f32[1792,128]{1,0:T(8,128)}, f32[1792,128]{1,0:T(8,128)}, f32[1792,128]{1,0:T(8,128)}) fusion(f32[1792,128]{1,0:T(8,128)S(1)} %bitcast.14, f32[1792,128]{1,0:T(8,128)S(1)} %get-tuple-element.15, f32[128]{0:T(128)S(1)} %bitcast.11, f32[1792,128]{1,0:T(8,128)S(1)} %bitcast.16, f32[1792,128]{1,0:T(8,128)S(1)} %bitcast.17), kind=kLoop, calls=%fused_computation.2 | loop fusion | flops 2981888 | bytes 6423040 | tf_op jit(solution)/shard_map/sub | solution.py:477
Async XLA Ops:
  0.6 73.1 %copy-start.2 = (f32[448,1,512]{2,1,0:T(1,128)S(1)}, f32[448,1,512]{2,1,0:T(1,128)}, u32[]{:S(2)}) copy-start(f32[448,1,512]{2,1,0:T(1,128)} %param.9) | copy-start | bytes 2752516
  0.6 73.1 %copy-start.1 = (f32[448,1,512]{2,1,0:T(1,128)S(1)}, f32[448,1,512]{2,1,0:T(1,128)}, u32[]{:S(2)}) copy-start(f32[448,1,512]{2,1,0:T(1,128)} %param.8) | copy-start | bytes 2752516
  0.7 73.1 %copy-start = (f32[448,1,512]{2,1,0:T(1,128)S(1)}, f32[448,1,512]{2,1,0:T(1,128)}, u32[]{:S(2)}) copy-start(f32[448,1,512]{2,1,0:T(1,128)} %param.7) | copy-start | bytes 2752516

commit v7 on v6

--- a/solution.py
+++ b/solution.py
@@ -44,6 +44,7 @@
     red_sem,
     mid1,
     mid2,
+    mid3,
 ):
     tok = a_v.shape[0]
     width = wbuf.shape[1]
@@ -153,8 +154,6 @@
         lax.fori_loop(0, width // 256, step, 0)
 
     X, UP, DOWN = (1, 0), (0, 1), (0, 3)
-    for who in near[-2:]:
-        pl.semaphore_signal(mid1, inc=1, device_id=who, device_id_type=MESH)
     with jax.named_scope("own"):
         for dest, q in (
             (X, 0), (UP, 2), (DOWN, 3), (X, 1), (UP, 3), (DOWN, 2),
@@ -228,8 +227,8 @@
             term = top + jnp.log(denom) - picked
             loss_lanes += jnp.sum(jnp.broadcast_to(term, (128, 128)), axis=0, keepdims=True)
 
-    pl.semaphore_wait(mid1, 2)
-    pl.semaphore_signal(mid2, inc=1, device_id={"layer": away}, device_id_type=MESH)
+    for who in near[-2:]:
+        pl.semaphore_signal(mid1, inc=1, device_id=who, device_id_type=MESH)
 
     def outer(left, right):
         return lax.dot_general(
@@ -325,6 +324,9 @@
 
     with jax.named_scope("rs_c1"):
         up_and_down(1)
+    pl.semaphore_wait(mid1, 2)
+    for who in near[-2:]:
+        pl.semaphore_signal(mid3, inc=1, device_id=who, device_id_type=MESH)
     with jax.named_scope("rs_d"):
         ship(two(UP, 2), partial(0, 2, 0) + got(x_first(2, 0), 0), UP)
         ship(two(DOWN, 2), partial(0, 2, 1) + got(x_first(2, 1), 1), DOWN)
@@ -334,7 +336,8 @@
         ship(one(UP, 2, 1), partial(0, 1, 1) + got(x_first(1, 1), 1), UP)
         ship(one(DOWN, 2, 0), partial(0, 3, 0) + got(x_first(3, 0), 0), DOWN)
     with jax.named_scope("rs_f"):
-        pl.semaphore_wait(mid2, 1)
+        pl.semaphore_wait(mid3, 2)
+        pl.semaphore_signal(mid2, inc=1, device_id={"layer": away}, device_id_type=MESH)
         for q in (3, 2):
             ship(x_last(q), partial(1, 0, q) + got(one(UP, 1, q), q) + got(one(DOWN, 1, q), q), X)
     with jax.named_scope("rs_g"):
@@ -357,6 +360,7 @@
         for q, side in ((1, UP), (0, DOWN)):
             total = partial(0, 0, q) + got(x_first(0, q), q) + got(one(side, 2, q), q)
             part[at(0, 0), block_rows(q), :] = total
+    pl.semaphore_wait(mid2, 1)
     with jax.named_scope("fin_b"):
         for q in (3, 2):
             square = finish(q, partial(0, 0, q) + got(x_last(q), q), square)
@@ -387,22 +391,24 @@
         all_sent(6 + stage, some)
         return jnp.sum(slots[...], axis=0)
 
-    m = y * 2 + c
-    n = x * 8 + lay
     with jax.named_scope("red1"):
-        tile = spread(
-            slots1, tile, m, [{"dp": x * 8 + (m + k) % 8} for k in range(1, 8)], 0
-        )
+        tile = spread(slots1, tile, c, [{"dp": dp_of(0, 0, 1)}], 0)
+        total = jnp.sum(tile[:, 0:128], axis=1, keepdims=True)
+        lower_lanes = lax.broadcasted_iota(jnp.int32, (1, 128), 1) < 64
+        tile = jnp.where(lower_lanes, jnp.broadcast_to(total, (1, 128)), tile[:, 128:256])
+    chips = [(i, j, k) for i in range(2) for j in range(4) for k in range(8) if i + j + k]
+    chips.sort(key=lambda o: -((0, 1, 2, 1)[o[1]] + (0, 1, 2, 1)[o[2] % 4] + (0, 1, 2, 1)[o[2] // 4 * 2 + o[0]]))
     with jax.named_scope("red2"):
-        others = [(n + k) % 16 for k in range(1, 16)]
+        index = (x * 4 + y) * 8 + lay
         sums = spread(
-            slots2, tile, n, [{"dp": o // 8 * 8 + m, "layer": o % 8} for o in others], 1
+            slots2, tile, index,
+            [{"dp": dp_of(i, j), "layer": ((lay // 4 + k // 4) % 2) * 4 + (lay + k) % 4} for i, j, k in chips], 1
         )
     with jax.named_scope("end1"):
         store.wait()
-    square = jnp.broadcast_to(jnp.sum(sums[:, 0:128], axis=1, keepdims=True), (1, 128))
+    square = jnp.broadcast_to(sums[:, 0:1], (1, 128))
     factor_ref[...] = jnp.minimum(1.0, 0.25 / jnp.sqrt(square + 1e-12))
-    loss_ref[...] = sums[:, 128:256] / (tokens * 8)
+    loss_ref[...] = jnp.broadcast_to(sums[:, 127:128], (1, 128)) / (tokens * 8)
 
 
 def shards(activations, labels, weights, first_moment, second_moment):
@@ -442,8 +448,8 @@
             vmem((28, 128, width), jnp.int16),
             vmem((28, 1, width), F32),
             vmem((65, 1, width), F32),
-            vmem((8, 1, 256), F32),
-            vmem((16, 1, 256), F32),
+            vmem((2, 1, 256), F32),
+            vmem((64, 1, 128), F32),
             dma((4,)),
             dma((8,)),
             dma((8, 4)),
@@ -452,6 +458,7 @@
             dma((1,)),
             dma((28,)),
             dma((2,)),
+            pltpu.SemaphoreType.REGULAR,
             pltpu.SemaphoreType.REGULAR,
             pltpu.SemaphoreType.REGULAR,
         ],

time: 77.1 us -> 76 us (0.986)
  Pallas kernels: 73.1 us -> 72 us
    pallas_call x1, Pallas kernels: 73.1 us -> 72 us  [shards(): pl.pallas_call(body, out_shape=(jax.ShapeDtypeStruct((lines, 128), F32),...]
where the time goes in v7:
time: 76 us; the launch traced here: 75.9 us
  Pallas kernels  72 us (95%)
  other arithmetic  1.96 us (3%)
  between operations  1.85 us (2%)
    pallas_call x1, Pallas kernels, shards(): pl.pallas_call(body, out_shape=(jax.ShapeDtypeStruct((lines, 128), F32),...  72 us
    sub x1, other arithmetic, shards(): weights - 0.001 * (new_first / (1.0 - 0.9 ** STEP)) / (jnp.sqrt(new_secon...  1.96 us

profile of v7, /device:TPU:1, one launch (start us, length us, event | category | flops | bytes accessed | tf_op | source)
XLA Modules:
  0.0 75.9 jit_solution(10675423102919333487)
XLA Ops:
  0.6 0.0 copy-start.2
  0.6 0.0 copy-start.1
  0.7 0.0 copy-start
  0.7 72.0 %probe_step.1 = (f32[1792,128]{1,0:T(8,128)S(1)}, f32[1,128]{1,0:T(1,128)S(1)}, f32[1,128]{1,0:T(1,128)S(1)}) custom-call(bf16[256,7168]{1,0:T(8,128)(2,1)} %bitcast.15, s32[2,128]{1,0:T(2,128)} %bitcast.21, f32[1792,128]{1,0:T(8,128)} %bitcast.13), custom_call_target="tpu_custom_call" | custom-call | tf_op jit(solution)/shard_map/probe_step/pallas_call | solution.py:428
  72.7 0.0 copy-done.2
  72.7 0.0 copy-done.1
  72.7 0.0 copy-done
  72.7 2.0 %divide_subtract_fusion = (f32[1792,128]{1,0:T(8,128)}, f32[1792,128]{1,0:T(8,128)}, f32[1792,128]{1,0:T(8,128)}) fusion(f32[1792,128]{1,0:T(8,128)S(1)} %bitcast.14, f32[1792,128]{1,0:T(8,128)S(1)} %get-tuple-element.15, f32[128]{0:T(128)S(1)} %bitcast.11, f32[1792,128]{1,0:T(8,128)S(1)} %bitcast.16, f32[1792,128]{1,0:T(8,128)S(1)} %bitcast.17), kind=kLoop, calls=%fused_computation.2 | loop fusion | flops 2981888 | bytes 6423040 | tf_op jit(solution)/shard_map/sub | solution.py:484
Async XLA Ops:
  0.6 72.1 %copy-start.2 = (f32[448,1,512]{2,1,0:T(1,128)S(1)}, f32[448,1,512]{2,1,0:T(1,128)}, u32[]{:S(2)}) copy-start(f32[448,1,512]{2,1,0:T(1,128)} %param.9) | copy-start | bytes 2752516
  0.6 72.1 %copy-start.1 = (f32[448,1,512]{2,1,0:T(1,128)S(1)}, f32[448,1,512]{2,1,0:T(1,128)}, u32[]{:S(2)}) copy-start(f32[448,1,512]{2,1,0:T(1,128)} %param.8) | copy-start | bytes 2752516
  0.7 72.1 %copy-start = (f32[448,1,512]{2,1,0:T(1,128)S(1)}, f32[448,1,512]{2,1,0:T(1,128)}, u32[]{:S(2)}) copy-start(f32[448,1,512]{2,1,0:T(1,128)} %param.7) | copy-start | bytes 2752516

commit v8 on v7

--- a/solution.py
+++ b/solution.py
@@ -198,14 +198,15 @@
         for q in (2, 3):
             w_take(1, 3, q)
             w_take(1, 1, q)
+        logits_of(1, 3)
+        logits_of(1, 1)
         w_take(0, 2, 0)
         w_take(0, 2, 1)
+    with jax.named_scope("relay6"):
+        for q in (2, 3, 0, 1):
+            w_take(1, 2, q)
+    with jax.named_scope("relay7"):
         logits_of(0, 2)
-        logits_of(1, 3)
-        logits_of(1, 1)
-    with jax.named_scope("relay6"):
-        for q in range(4):
-            w_take(1, 2, q)
         logits_of(1, 2)
 
     with jax.named_scope("softmax"):

time: 76 us -> 74.2 us (0.976)
  Pallas kernels: 72 us -> 70.2 us
    pallas_call x1, Pallas kernels: 72 us -> 70.2 us  [shards(): pl.pallas_call(body, out_shape=(jax.ShapeDtypeStruct((lines, 128), F32),...]
where the time goes in v8:
time: 74.2 us; the launch traced here: 74 us
  Pallas kernels  70.2 us (95%)
  other arithmetic  1.96 us (3%)
  between operations  1.85 us (2%)
    pallas_call x1, Pallas kernels, shards(): pl.pallas_call(body, out_shape=(jax.ShapeDtypeStruct((lines, 128), F32),...  70.2 us
    sub x1, other arithmetic, shards(): weights - 0.001 * (new_first / (1.0 - 0.9 ** STEP)) / (jnp.sqrt(new_secon...  1.96 us

profile of v8, /device:TPU:1, one launch (start us, length us, event | category | flops | bytes accessed | tf_op | source)
XLA Modules:
  0.0 74.0 jit_solution(13213997096192365162)
XLA Ops:
  0.6 0.0 copy-start.2
  0.6 0.0 copy-start.1
  0.7 0.0 copy-start
  0.7 70.2 %probe_step.1 = (f32[1792,128]{1,0:T(8,128)S(1)}, f32[1,128]{1,0:T(1,128)S(1)}, f32[1,128]{1,0:T(1,128)S(1)}) custom-call(bf16[256,7168]{1,0:T(8,128)(2,1)} %bitcast.15, s32[2,128]{1,0:T(2,128)} %bitcast.21, f32[1792,128]{1,0:T(8,128)} %bitcast.13), custom_call_target="tpu_custom_call" | custom-call | tf_op jit(solution)/shard_map/probe_step/pallas_call | solution.py:429
  70.9 0.0 copy-done.2
  70.9 0.0 copy-done.1
  70.9 0.0 copy-done
  70.9 2.0 %divide_subtract_fusion = (f32[1792,128]{1,0:T(8,128)}, f32[1792,128]{1,0:T(8,128)}, f32[1792,128]{1,0:T(8,128)}) fusion(f32[1792,128]{1,0:T(8,128)S(1)} %bitcast.14, f32[1792,128]{1,0:T(8,128)S(1)} %get-tuple-element.15, f32[128]{0:T(128)S(1)} %bitcast.11, f32[1792,128]{1,0:T(8,128)S(1)} %bitcast.16, f32[1792,128]{1,0:T(8,128)S(1)} %bitcast.17), kind=kLoop, calls=%fused_computation.2 | loop fusion | flops 2981888 | bytes 6423040 | tf_op jit(solution)/shard_map/sub | solution.py:485
Async XLA Ops:
  0.6 70.3 %copy-start.2 = (f32[448,1,512]{2,1,0:T(1,128)S(1)}, f32[448,1,512]{2,1,0:T(1,128)}, u32[]{:S(2)}) copy-start(f32[448,1,512]{2,1,0:T(1,128)} %param.9) | copy-start | bytes 2752516
  0.6 70.3 %copy-start.1 = (f32[448,1,512]{2,1,0:T(1,128)S(1)}, f32[448,1,512]{2,1,0:T(1,128)}, u32[]{:S(2)}) copy-start(f32[448,1,512]{2,1,0:T(1,128)} %param.8) | copy-start | bytes 2752516
  0.7 70.3 %copy-start = (f32[448,1,512]{2,1,0:T(1,128)S(1)}, f32[448,1,512]{2,1,0:T(1,128)}, u32[]{:S(2)}) copy-start(f32[448,1,512]{2,1,0:T(1,128)} %param.7) | copy-start | bytes 2752516

commit v9 on v8

--- a/solution.py
+++ b/solution.py
@@ -223,11 +223,10 @@
             picked = jnp.sum(logits * onehot, axis=1, keepdims=True)
             probs = exps / denom
             slopes[0, t * 128 : (t + 1) * 128, :] = ((probs - onehot) / tokens).astype(BF16)
-            half = slopes.at[0, pl.ds(t * 128, 128), :]
-            send(3, half, slopes.at[1, pl.ds(t * 128, 128), :], sr_sem.at[0], dp_of(0, 0, 1))
             term = top + jnp.log(denom) - picked
             loss_lanes += jnp.sum(jnp.broadcast_to(term, (128, 128)), axis=0, keepdims=True)
 
+    send(3, slopes.at[0], slopes.at[1], sr_sem.at[0], dp_of(0, 0, 1))
     for who in near[-2:]:
         pl.semaphore_signal(mid1, inc=1, device_id=who, device_id_type=MESH)
 

time: 74.2 us -> 73.9 us (level)
  no operation moved by 1% of the time
where the time goes in v9:
time: 73.9 us; the launch traced here: 73.8 us
  Pallas kernels  70 us (95%)
  other arithmetic  1.96 us (3%)
  between operations  1.85 us (3%)
    pallas_call x1, Pallas kernels, shards(): pl.pallas_call(body, out_shape=(jax.ShapeDtypeStruct((lines, 128), F32),...  70 us
    sub x1, other arithmetic, shards(): weights - 0.001 * (new_first / (1.0 - 0.9 ** STEP)) / (jnp.sqrt(new_secon...  1.96 us

profile of v9, /device:TPU:1, one launch (start us, length us, event | category | flops | bytes accessed | tf_op | source)
XLA Modules:
  0.0 73.8 jit_solution(12923967981596518283)
XLA Ops:
  0.6 0.0 copy-start.2
  0.6 0.0 copy-start.1
  0.7 0.0 copy-start
  0.7 70.0 %probe_step.1 = (f32[1792,128]{1,0:T(8,128)S(1)}, f32[1,128]{1,0:T(1,128)S(1)}, f32[1,128]{1,0:T(1,128)S(1)}) custom-call(bf16[256,7168]{1,0:T(8,128)(2,1)} %bitcast.15, s32[2,128]{1,0:T(2,128)} %bitcast.21, f32[1792,128]{1,0:T(8,128)} %bitcast.13), custom_call_target="tpu_custom_call" | custom-call | tf_op jit(solution)/shard_map/probe_step/pallas_call | solution.py:428
  70.7 0.0 copy-done.2
  70.7 0.0 copy-done.1
  70.7 0.0 copy-done
  70.7 2.0 %divide_subtract_fusion = (f32[1792,128]{1,0:T(8,128)}, f32[1792,128]{1,0:T(8,128)}, f32[1792,128]{1,0:T(8,128)}) fusion(f32[1792,128]{1,0:T(8,128)S(1)} %bitcast.14, f32[1792,128]{1,0:T(8,128)S(1)} %get-tuple-element.15, f32[128]{0:T(128)S(1)} %bitcast.11, f32[1792,128]{1,0:T(8,128)S(1)} %bitcast.16, f32[1792,128]{1,0:T(8,128)S(1)} %bitcast.17), kind=kLoop, calls=%fused_computation.2 | loop fusion | flops 2981888 | bytes 6423040 | tf_op jit(solution)/shard_map/sub | solution.py:484
Async XLA Ops:
  0.6 70.0 %copy-start.2 = (f32[448,1,512]{2,1,0:T(1,128)S(1)}, f32[448,1,512]{2,1,0:T(1,128)}, u32[]{:S(2)}) copy-start(f32[448,1,512]{2,1,0:T(1,128)} %param.9) | copy-start | bytes 2752516
  0.6 70.0 %copy-start.1 = (f32[448,1,512]{2,1,0:T(1,128)S(1)}, f32[448,1,512]{2,1,0:T(1,128)}, u32[]{:S(2)}) copy-start(f32[448,1,512]{2,1,0:T(1,128)} %param.8) | copy-start | bytes 2752516
  0.7 70.0 %copy-start = (f32[448,1,512]{2,1,0:T(1,128)S(1)}, f32[448,1,512]{2,1,0:T(1,128)}, u32[]{:S(2)}) copy-start(f32[448,1,512]{2,1,0:T(1,128)} %param.7) | copy-start | bytes 2752516
